TPU v7x, 32 devices: a whole 2x2x4 slice. The times are simulated.
32 devices in a mesh: ep: 8 (over z, x), corner: 4 (over y, core).
Axes of the slice: x: 2, y: 2, z: 4, core: 2. Of those that a mesh axis runs over, the one named last changes fastest.
Arguments:
- required: float32 [8, 262144], P('corner', 'ep'), may hold values from -3 to 3
- arrival: float32 [8, 262144], P('corner', 'ep'), may hold values from -7.2 to 7.2
- hold_required: float32 [8, 262144], P('corner', 'ep'), may hold values from -5.4 to 5.4
- early_arrival: float32 [8, 262144], P('corner', 'ep'), may hold values from -3 to 3
- part_ids: int32 [262144], P('ep'), may hold values from 0 to 63
- bin_edges: int32 [512], replicated, may hold values from -4096 to -1, as said below
Outputs:
- part_hist: float32 [64, 8, 2, 512], P(None, 'corner')
- part_tns: float32 [64, 8, 2], P(None, 'corner')
- part_share: float32 [64], replicated
- tns: float32 [8, 2], P('corner')
- wns: float32 [8, 2], P('corner')
- worst: float32 [2, 262144], P(None, 'ep')
Inputs may be any that keep to these rules, and one draw needn't show every extreme that they name: `bin_edges`: strictly increasing and negative; consecutive nodes differ by 1 to 8.
All inputs are finite; a program needn't handle non-finite values.
Results may differ from a plain program's by a relative error of at most 0.0003.
Values sent between devices are 32-bit elements; how exact they have to be, the bound alone decides.
No kernel may reach another device: no remote copies, remote signals or barrier semaphores. Data moves between devices by JAX's collectives and lax.ppermute only.
A program may use at most 64 MiB of HBM per device.

v0:
```python
import jax
import jax.numpy as jnp
from jax import lax
from jax.sharding import PartitionSpec as P

GROUPS = 64


def node_tables(bin_edges):
    nodes = bin_edges.astype(jnp.float32) * 0.001
    upper = jnp.concatenate([nodes[1:], jnp.zeros((1,), jnp.float32)])
    lower = jnp.concatenate([nodes[:1] - 1.0, nodes[:-1]])
    return (nodes, lower, upper)


def on_device(required, arrival, hold_required, early_arrival, part_ids, bin_edges):
    corner_count, rows = required.shape
    endpoints = rows * lax.axis_size("ep")
    nodes, lower, upper = node_tables(bin_edges)
    setup = required - arrival
    hold = early_arrival - hold_required
    worst_pair = lax.pmin((jnp.min(setup, axis=0), jnp.min(hold, axis=0)), "corner")
    worst = jnp.stack(worst_pair, axis=0)
    both = jnp.stack([setup, hold], axis=1)
    block = min(4096, rows)
    labels = jnp.arange(GROUPS, dtype=jnp.int32)
    node_col = nodes[None, :, None]
    low_col = lower[None, :, None]
    high_col = upper[None, :, None]
    rise_den = node_col - low_col
    fall_den = high_col - node_col
    contract = (((1,), (1,)), ((), ()))

    def one_block(index, carry):
        hist, stats, counts = carry
        start = index * block
        ids_block = lax.dynamic_slice_in_dim(part_ids, start, block, 0)
        member = labels[:, None] == ids_block[None, :]
        member_low = member.astype(jnp.bfloat16)
        member_full = member.astype(jnp.float32)
        slab = lax.dynamic_slice_in_dim(both, start, block, 2)
        level = jnp.clip(slab, nodes[0], 0.0).reshape(corner_count * 2, 1, block)
        weight = jnp.maximum(
            jnp.minimum((level - low_col) / rise_den, (high_col - level) / fall_den), 0.0
        )
        weight = weight.astype(jnp.bfloat16)
        product = jnp.einsum("pe,kbe->pkb", member_low, weight, preferred_element_type=jnp.float32)
        hist = hist + product.reshape(GROUPS, corner_count, 2, nodes.shape[0])
        negative = jnp.minimum(slab, 0.0).reshape(corner_count * 2, block)
        part_neg = lax.dot_general(
            member_full,
            negative,
            contract,
            precision=lax.Precision.HIGHEST,
            preferred_element_type=jnp.float32,
        )
        stats = stats + part_neg.reshape(GROUPS, corner_count, 2)
        counts = counts + jnp.sum(member_full, axis=1)
        return (hist, stats, counts)

    start_state = (
        jnp.zeros((GROUPS, corner_count, 2, nodes.shape[0]), jnp.float32),
        jnp.zeros((GROUPS, corner_count, 2), jnp.float32),
        jnp.zeros((GROUPS,), jnp.float32),
    )
    hist, stats, counts = lax.fori_loop(0, rows // block, one_block, start_state)
    local_min = jnp.stack([jnp.min(setup, axis=1), jnp.min(hold, axis=1)], axis=1)
    wns = lax.pmin(local_min, "ep")
    hist, stats, counts = lax.psum((hist, stats, counts), "ep")
    tns_raw = jnp.sum(stats, axis=0)
    density = GROUPS * nodes.shape[0] / endpoints
    share = GROUPS / endpoints
    part_hist = hist * density
    part_tns = stats * share
    part_share = counts * share
    tns = tns_raw * (1.0 / endpoints)
    return (part_hist, part_tns, part_share, tns, wns, worst)


def solution(mesh):
    in_specs = (
        P("corner", "ep"),
        P("corner", "ep"),
        P("corner", "ep"),
        P("corner", "ep"),
        P("ep"),
        P(),
    )
    out_specs = (
        P(None, "corner", None, None),
        P(None, "corner", None),
        P(),
        P("corner", None),
        P("corner", None),
        P(None, "ep"),
    )
    return jax.shard_map(
        on_device, mesh=mesh, in_specs=in_specs, out_specs=out_specs, check_vma=False
    )
```

profile of v0, /device:TPU:0, one launch (start us, length us, event | category | flops | bytes accessed | tf_op | source)
XLA Modules:
  0.0 186.4 jit_solution(7004410176938454817)
XLA Ops:
  7.2 2.9 %fusion.19 = (f32[32768]{0:T(1024)}, f32[2]{0:T(128)}, f32[2,32768]{1,0:T(2,128)S(1)}, f32[2]{0:T(128)}, f32[32768]{0:T(1024)}, /*index=5*/f32[2,32768]{1,0:T(2,128)S(1)}) fusion(f32[2,32768]{1,0:T(2,128)} %param.8, f32[2,32768]{1,0:T(2,128)} %param.9, f32[2,32768]{1,0:T(2,128)} %param.11, f32[2,32768]{1,0:T(2,128)} %param.10), kind=kLoop, calls=%fused_computation.32 | loop fusion | flops 327676 | bytes 1835024 | tf_op jit(solution)/shard_map/reduce_min | solution.py:22
  10.2 0.5 slice.16
  10.8 0.2 stack.27
  11.0 0.2 stack.28
  11.8 0.5 pad_maximum_fusion
  12.4 88.2 %while.18 = (s32[]{:T(128)}, f32[64,2,2,512]{3,0,2,1:T(8,128)S(1)}, f32[64,2,2]{0,2,1:T(2,128)S(1)}, f32[64]{0:T(128)S(1)}, s32[32768]{0:T(1024)}, /*index=5*/f3...) while((s32[]{:T(128)}, f32[64,2,2,512]{3,0,2,1:T(8,128)S(1)}, ...), condition=%wide.region_2.0_spmd.clone, body=%wide.region_0.2_spmd.clone.sunk | while | flops 1146667648 | bytes 2584807 | solution.py:66
  12.4 0.5 slice.23
  12.9 0.7 dynamic_slice.26
  13.6 0.2 fusion.33
  13.8 0.6 convolution_add_fusion.2
  14.5 0.7 maximum_minimum_fusion.2
  15.2 8.0 %fusion.32 = f32[64,4,512]{2,0,1:T(8,128)S(1)} fusion(f32[512]{0:T(512)S(1)} %bitcast.40, f32[512]{0:T(512)S(1)} %bitcast.42, f32[512]{0:T(512)S(1)} %bitcast.44, f32[512]{0:T(512)S(1)} %bitcast.46, f32[4,4096]{1,0:T(4,128)S(1)} %sub.129, s32[4096]{0:T(1024)S(1)} %dynamic_slice.26), kind=kOutput, calls=%fused_computation.2.clone.1 | convolution fusion | flops 1132724224 | bytes 614400 | tf_op jit(solution)/shard_map/while/body/eval_jaxpr/pe,kbe->pkb/dot_general | solution.py:47
  23.4 0.5 slice.23
  23.9 0.7 dynamic_slice.26
  24.6 0.2 fusion.33
  24.9 0.6 convolution_add_fusion.2
  25.5 0.7 maximum_minimum_fusion.2
  26.3 8.0 %fusion.32 = f32[64,4,512]{2,0,1:T(8,128)S(1)} fusion(f32[512]{0:T(512)S(1)} %bitcast.40, f32[512]{0:T(512)S(1)} %bitcast.42, f32[512]{0:T(512)S(1)} %bitcast.44, f32[512]{0:T(512)S(1)} %bitcast.46, f32[4,4096]{1,0:T(4,128)S(1)} %sub.129, s32[4096]{0:T(1024)S(1)} %dynamic_slice.26), kind=kOutput, calls=%fused_computation.2.clone.1 | convolution fusion | flops 1132724224 | bytes 614400 | tf_op jit(solution)/shard_map/while/body/eval_jaxpr/pe,kbe->pkb/dot_general | solution.py:47
  34.4 0.5 slice.23
  34.9 0.7 dynamic_slice.26
  35.7 0.2 fusion.33
  35.9 0.6 convolution_add_fusion.2
  36.5 0.7 maximum_minimum_fusion.2
  37.3 8.0 %fusion.32 = f32[64,4,512]{2,0,1:T(8,128)S(1)} fusion(f32[512]{0:T(512)S(1)} %bitcast.40, f32[512]{0:T(512)S(1)} %bitcast.42, f32[512]{0:T(512)S(1)} %bitcast.44, f32[512]{0:T(512)S(1)} %bitcast.46, f32[4,4096]{1,0:T(4,128)S(1)} %sub.129, s32[4096]{0:T(1024)S(1)} %dynamic_slice.26), kind=kOutput, calls=%fused_computation.2.clone.1 | convolution fusion | flops 1132724224 | bytes 614400 | tf_op jit(solution)/shard_map/while/body/eval_jaxpr/pe,kbe->pkb/dot_general | solution.py:47
  45.5 0.5 slice.23
  46.0 0.7 dynamic_slice.26
  46.7 0.2 fusion.33
  46.9 0.6 convolution_add_fusion.2
  47.6 0.7 maximum_minimum_fusion.2
  48.3 8.0 %fusion.32 = f32[64,4,512]{2,0,1:T(8,128)S(1)} fusion(f32[512]{0:T(512)S(1)} %bitcast.40, f32[512]{0:T(512)S(1)} %bitcast.42, f32[512]{0:T(512)S(1)} %bitcast.44, f32[512]{0:T(512)S(1)} %bitcast.46, f32[4,4096]{1,0:T(4,128)S(1)} %sub.129, s32[4096]{0:T(1024)S(1)} %dynamic_slice.26), kind=kOutput, calls=%fused_computation.2.clone.1 | convolution fusion | flops 1132724224 | bytes 614400 | tf_op jit(solution)/shard_map/while/body/eval_jaxpr/pe,kbe->pkb/dot_general | solution.py:47
  56.5 0.5 slice.23
  57.0 0.7 dynamic_slice.26
  57.7 0.2 fusion.33
  57.9 0.6 convolution_add_fusion.2
  58.6 0.7 maximum_minimum_fusion.2
  59.3 8.0 %fusion.32 = f32[64,4,512]{2,0,1:T(8,128)S(1)} fusion(f32[512]{0:T(512)S(1)} %bitcast.40, f32[512]{0:T(512)S(1)} %bitcast.42, f32[512]{0:T(512)S(1)} %bitcast.44, f32[512]{0:T(512)S(1)} %bitcast.46, f32[4,4096]{1,0:T(4,128)S(1)} %sub.129, s32[4096]{0:T(1024)S(1)} %dynamic_slice.26), kind=kOutput, calls=%fused_computation.2.clone.1 | convolution fusion | flops 1132724224 | bytes 614400 | tf_op jit(solution)/shard_map/while/body/eval_jaxpr/pe,kbe->pkb/dot_general | solution.py:47
  67.5 0.5 slice.23
  68.0 0.7 dynamic_slice.26
  68.7 0.2 fusion.33
  69.0 0.6 convolution_add_fusion.2
  69.6 0.7 maximum_minimum_fusion.2
  70.4 8.0 %fusion.32 = f32[64,4,512]{2,0,1:T(8,128)S(1)} fusion(f32[512]{0:T(512)S(1)} %bitcast.40, f32[512]{0:T(512)S(1)} %bitcast.42, f32[512]{0:T(512)S(1)} %bitcast.44, f32[512]{0:T(512)S(1)} %bitcast.46, f32[4,4096]{1,0:T(4,128)S(1)} %sub.129, s32[4096]{0:T(1024)S(1)} %dynamic_slice.26), kind=kOutput, calls=%fused_computation.2.clone.1 | convolution fusion | flops 1132724224 | bytes 614400 | tf_op jit(solution)/shard_map/while/body/eval_jaxpr/pe,kbe->pkb/dot_general | solution.py:47
  78.5 0.5 slice.23
  79.0 0.7 dynamic_slice.26
  79.8 0.2 fusion.33
  80.0 0.6 convolution_add_fusion.2
  80.6 0.7 maximum_minimum_fusion.2
  81.4 8.0 %fusion.32 = f32[64,4,512]{2,0,1:T(8,128)S(1)} fusion(f32[512]{0:T(512)S(1)} %bitcast.40, f32[512]{0:T(512)S(1)} %bitcast.42, f32[512]{0:T(512)S(1)} %bitcast.44, f32[512]{0:T(512)S(1)} %bitcast.46, f32[4,4096]{1,0:T(4,128)S(1)} %sub.129, s32[4096]{0:T(1024)S(1)} %dynamic_slice.26), kind=kOutput, calls=%fused_computation.2.clone.1 | convolution fusion | flops 1132724224 | bytes 614400 | tf_op jit(solution)/shard_map/while/body/eval_jaxpr/pe,kbe->pkb/dot_general | solution.py:47
  89.6 0.5 slice.23
  90.1 0.7 dynamic_slice.26
  90.8 0.2 fusion.33
  91.0 0.6 convolution_add_fusion.2
  91.6 0.7 maximum_minimum_fusion.2
  92.4 8.0 %fusion.32 = f32[64,4,512]{2,0,1:T(8,128)S(1)} fusion(f32[512]{0:T(512)S(1)} %bitcast.40, f32[512]{0:T(512)S(1)} %bitcast.42, f32[512]{0:T(512)S(1)} %bitcast.44, f32[512]{0:T(512)S(1)} %bitcast.46, f32[4,4096]{1,0:T(4,128)S(1)} %sub.129, s32[4096]{0:T(1024)S(1)} %dynamic_slice.26), kind=kOutput, calls=%fused_computation.2.clone.1 | convolution fusion | flops 1132724224 | bytes 614400 | tf_op jit(solution)/shard_map/while/body/eval_jaxpr/pe,kbe->pkb/dot_general | solution.py:47
  100.6 1.2 copy.12
  101.8 23.5 %pmin.21 = f32[2,2]{0,1:T(2,128)S(1)} all-reduce(f32[2,2]{0,1:T(2,128)S(1)} %pad_maximum_fusion.4), channel_id=1, replica_groups=mesh['ep'=8,'corner'=4] {'ep'}, use_global_device_ids=true, to_apply=%region_9.10 | all-reduce | flops 4 | bytes 32 | tf_op jit(solution)/shard_map/pmin | solution.py:68
  125.3 0.7 copy.13
  126.0 17.2 %all-reduce = (f32[64,2,2]{0,2,1:T(2,128)S(1)}, f32[64]{0:T(128)S(1)}) all-reduce(f32[64,2,2]{0,2,1:T(2,128)S(1)} %get-tuple-element.208, f32[64]{0:T(128)S(1)} %get-tuple-element.209), channel_id=1, replica_groups=mesh['ep'=8,'corner'=4] {'ep'}, use_global_device_ids=true, to_apply=%region_4.5 | all-reduce | flops 320 | bytes 2560 | tf_op jit(solution)/shard_map/psum | solution.py:69
  143.2 0.5 broadcast_multiply_fusion.3
  143.7 0.6 fusion.21
  144.3 0.6 broadcast_multiply_fusion.2
  144.9 1.9 %pad_maximum_fusion.1 = f32[2,32768]{1,0:T(2,128)} fusion(f32[1,32768]{1,0:T(1,128)} %get-tuple-element.282, f32[1,32768]{1,0:T(1,128)} %get-tuple-element.283), kind=kLoop, calls=%fused_computation.21 | loop fusion | flops 65536 | bytes 524288 | tf_op jit(solution)/shard_map/stack | solution.py:23
  146.8 30.8 %all-reduce.5.cloned.1.call-done = f32[64,2,2,512]{3,2,1,0:T(2,128)} async-done(((f32[64,2,2,512]{3,2,1,0:T(2,128)}), f32[64,2,2,512]{3,2,1,0:T(2,128)}) %all-reduce.5.cloned.1.call-update) | async-done | bytes 524304 | tf_op jit(solution)/shard_map/psum | solution.py:69
  177.5 2.1 %broadcast_multiply_fusion = f32[64,2,2,512]{3,2,1,0:T(2,128)} fusion(f32[64,2,2,512]{3,2,1,0:T(2,128)} %all-reduce.5.cloned.1.call-done), kind=kLoop, calls=%fused_computation.22 | loop fusion | flops 131072 | bytes 1048576 | tf_op jit(solution)/shard_map/mul | solution.py:73
  (42 shorter events, 2.3 us)
Async XLA Ops:
  7.2 3.0 %copy-start = (s32[512]{0:T(512)S(1)}, s32[512]{0:T(512)}, u32[]{:S(2)}) copy-start(s32[512]{0:T(512)} %param.13) | copy-start | bytes 6148
  7.2 137.7 %all-reduce.7.cloned.1.call-start = ((), (), s32[]{:S(2)}) async-start(), calls=%async_computation.1 | async-start | bytes 524288 | tf_op jit(solution)/shard_map/pmin | solution.py:22
  10.1 167.4 %all-reduce.5.cloned.1.call-start = ((), (), s32[]{:S(2)}) async-start(), calls=%async_computation | async-start | bytes 1048576 | tf_op jit(solution)/shard_map/psum | solution.py:69
  100.6 1.2 copy-start.1
  100.6 1.2 copy-start.2
Sparse Core Ops, SparseCore 0:
  11.0 35.2 all-reduce.6
  101.9 75.5 all-reduce.4
where the time goes:
time: 187 us; the launch traced here: 186 us
  matrix products  68.7 us (37%)
  blocking collectives  40.7 us (22%)
  waiting for transfers between devices  30.8 us (16%)
  other arithmetic  17.8 us (10%)
  between operations  14.8 us (8%)
  local copies, waits for them, and re-layouts  13.1 us (7%)
    dot_general x8, matrix products, one_block(): jnp.einsum('pe,kbe->pkb', member_low, weight, preferred_element_type=jnp....  63.7 us
    psum x1, waiting for transfers between devices, on_device(): hist, stats, counts = lax.psum((hist, stats, counts), 'ep')  30.8 us
    pmin x1, blocking collectives, on_device(): wns = lax.pmin(local_min, 'ep')  23.5 us
    psum x1, blocking collectives, on_device(): hist, stats, counts = lax.psum((hist, stats, counts), 'ep')  17.2 us
    dynamic_slice x8, local copies, waits for them, and re-layouts, one_block(): ids_block = lax.dynamic_slice_in_dim(part_ids, start, block, 0)  5.75 us
    min x8, other arithmetic, one_block(): level = jnp.clip(slab, nodes[0], 0.0).reshape(corner_count * 2, 1, block)  5.49 us
    dot_general x8, matrix products, one_block(): lax.dot_general(member_full, negative, contract, precision=lax.Precision....  5.07 us
    slice x8, local copies, waits for them, and re-layouts, one_block(): level = jnp.clip(slab, nodes[0], 0.0).reshape(corner_count * 2, 1, block)  4.11 us
  transfers between devices with their start and end apart: 2, of which 1 were waited for; matrix products, arithmetic and copies ran while one was open for 51% of the time, Pallas kernels for 0%

commit v1 on v0

v1 whole, which is shorter than its diff:
```python
import functools
import jax
import jax.numpy as jnp
from jax import lax
from jax.experimental import pallas as pl
from jax.experimental.pallas import tpu as pltpu
from jax.sharding import PartitionSpec as P

GROUPS = 64
LANES = 128
LEAST = 4096
F8 = jnp.float8_e4m3fn
BF = jnp.bfloat16
STEP = 0.001


def lookup(table_ref, index):
    lane = index & (LANES - 1)
    row = index >> 7
    out = None
    for r in range(table_ref.shape[0]):
        line = jnp.broadcast_to(table_ref[r:r + 1, :], index.shape)
        got = jnp.take_along_axis(line, lane, axis=1, mode="promise_in_bounds")
        out = got if out is None else jnp.where(row == r, got, out)
    return out


def interval(slack, x0, coarse_ref, fine_ref):
    t = jnp.minimum(jnp.maximum(slack, x0), 0.0)
    whole = jnp.floor(t * 1000.0)
    whole = jnp.where(t >= (whole + 1.0) * jnp.float32(STEP), whole + 1.0, whole)
    whole = jnp.where(t < whole * jnp.float32(STEP), whole - 1.0, whole)
    q = jnp.minimum(whole.astype(jnp.int32) + LEAST, LEAST - 1)
    cell = lookup(coarse_ref, q >> 3)
    upto = jnp.left_shift(2, q & 7) - 1
    j = (cell & 0xFFFF) + lax.population_count((cell >> 16) & upto) - 1
    pair = lookup(fine_ref, j)
    k = (pair & 0xFFFF) - LEAST
    x = k.astype(jnp.float32) * jnp.float32(STEP)
    xn = (k + (pair >> 16)).astype(jnp.float32) * jnp.float32(STEP)
    r = 1.0 / (xn - x)
    w1 = jnp.maximum((xn - t) * r, 0.0)
    w2 = jnp.maximum((t - x) * r, 0.0)
    local = j & (LANES - 1)
    odd = (j & 1) == 1
    even_place = ((local + 1) & ~1).astype(jnp.float32)
    odd_place = (local | 1).astype(jnp.float32)
    return (
        even_place,
        odd_place,
        jnp.where(odd, w2, w1),
        jnp.where(odd, w1, w2),
        (j >> 7).astype(jnp.float32),
        jnp.minimum(slack, 0.0),
    )


def prep_kernel(C, edges_ref, lines_ref, a_ref, b_ref, c_ref, d_ref, coarse_ref, fine_ref, worst_ref, low_ref):
    bins = edges_ref.shape[0]
    cell = lax.broadcasted_iota(jnp.int32, coarse_ref.shape, 0) * LANES + lax.broadcasted_iota(
        jnp.int32, coarse_ref.shape, 1
    )
    zero = jnp.zeros(coarse_ref.shape, jnp.int32)

    def add(i, state):
        state = list(state)
        for u in range(16):
            q = edges_ref[i * 16 + u] + LEAST
            here = q >> 3
            base, bits = state[u % 4]
            base = base + jnp.where(cell > here, 1, 0)
            bits = bits + jnp.where(cell == here, jnp.left_shift(65536, q & 7), 0)
            state[u % 4] = (base, bits)
        return tuple(state)

    state = lax.fori_loop(0, bins // 16, add, tuple((zero, zero) for _ in range(4)))
    coarse_ref[...] = sum(base + bits for base, bits in state)
    q = lines_ref[...] + LEAST
    _, lanes = q.shape
    left = pltpu.roll(q, lanes - 1, 1)
    below = jnp.concatenate([left[1:], jnp.full((1, lanes), LEAST, jnp.int32)], axis=0)
    last = lax.broadcasted_iota(jnp.int32, q.shape, 1) == lanes - 1
    following = jnp.where(last, below, left)
    fine_ref[...] = q + (following - q) * 65536

    setup = a_ref[...] - b_ref[...]
    hold = c_ref[...] - d_ref[...]
    size = setup.shape[0]
    for m, slack in enumerate((setup, hold)):
        low_ref[m] = jnp.min(slack.reshape(size // 8, 8, LANES), axis=0)
    first = lax.broadcasted_iota(jnp.int32, setup.shape, 0) % C == 0
    for m, slack in enumerate((setup, hold)):
        least = slack
        for c in range(1, C):
            least = jnp.minimum(least, pltpu.roll(slack, size - c, 0))
        if m:
            least = pltpu.roll(least, 1, 0)
            worst_ref[...] = jnp.where(first, worst_ref[...], least)
        else:
            worst_ref[...] = least


def run_prep(edges, a, b, c, d, C):
    bins = edges.shape[0]
    return pl.pallas_call(
        functools.partial(prep_kernel, C),
        in_specs=[pl.BlockSpec(memory_space=pltpu.SMEM)] + [pl.BlockSpec(memory_space=pltpu.VMEM)] * 5,
        out_shape=[
            jax.ShapeDtypeStruct((LEAST // 8 // LANES, LANES), jnp.int32),
            jax.ShapeDtypeStruct((bins // LANES, LANES), jnp.int32),
            jax.ShapeDtypeStruct(a.shape, jnp.float32),
            jax.ShapeDtypeStruct((2, 8, LANES), jnp.float32),
        ],
        name="prep",
    )(edges, edges.reshape(-1, LANES), a, b, c, d)


def hist_kernel(C, KT, n, edges_ref, coarse_ref, fine_ref, ids_ref, a_ref, b_ref, c_ref, d_ref, low_ref, out_ref, buf0, buf1):
    series = 2 * C
    nblk = fine_ref.shape[0]
    lines = KT * C
    chunks = ids_ref.shape[0] // KT
    own = GROUPS // n
    x0 = edges_ref[0].astype(jnp.float32) * jnp.float32(STEP)

    def body(*accs):
        for a in accs:
            pltpu.matmul_pop(a)
        iota16 = lax.broadcasted_iota(jnp.int32, (16, LANES), 0)
        iotas = [(iota16 + 16 * v).astype(jnp.float32).astype(BF) for v in range(LANES // 16)]
        iota32 = lax.broadcasted_iota(jnp.int32, (32, LANES), 0)
        iotas32 = [(iota32 + 32 * v).astype(jnp.float32).astype(BF) for v in range(GROUPS // 32)]
        even = (iota16 & 1) == 0
        iota8 = lax.broadcasted_iota(jnp.int32, (8, LANES), 0)
        one = jnp.ones((32, LANES), BF)
        zero16 = jnp.zeros((16, LANES), BF)
        zero32 = jnp.zeros((32, LANES), BF)
        none = jnp.zeros((32, LANES), F8)
        tail = jnp.where(iota8 == 3, 1.0, 0.0)

        def wide(x, rows):
            return jnp.broadcast_to(x, (rows, LANES))

        def look(buf, chunk, g):
            start = pl.multiple_of(chunk * lines + g * 8, 8)
            at = pl.ds(start, 8)
            for m, slack in enumerate((a_ref[at, :] - b_ref[at, :], c_ref[at, :] - d_ref[at, :])):
                for i, v in enumerate(interval(slack, x0, coarse_ref, fine_ref)):
                    buf[i, m, g * 8:g * 8 + 8, :] = v

        def pair(buf, chunk, k2):
            member = []
            for kk in range(2):
                ids = wide(ids_ref[pl.ds(chunk * KT + 2 * k2 + kk, 1), :], 32).astype(jnp.float32).astype(BF)
                member.append([jnp.where(i == ids, one, zero32).astype(F8) for i in iotas32])
            for s in range(series):
                c, m = divmod(s, 2)
                left, right = [], []
                for kk in range(2):
                    r = (2 * k2 + kk) * C + c
                    row = [buf[i, m, r:r + 1, :] for i in range(6)]
                    block = wide(row[4], 32).astype(BF)
                    left.append(jnp.concatenate([
                        jnp.where(block == jnp.bfloat16(h), part, none) for h in range(nblk) for part in member[kk]
                    ], axis=0))
                    place = jnp.where(even, wide(row[0], 16), wide(row[1], 16)).astype(BF)
                    weight = jnp.where(even, wide(row[2], 16), wide(row[3], 16)).astype(BF)
                    hats = [jnp.where(i == place, weight, zero16) for i in iotas]
                    negative = wide(row[5], 8)
                    high = negative.astype(BF).astype(jnp.float32)
                    cross = jnp.where(wide(row[0], 8) == float(LANES), wide(row[2], 8), 0.0)
                    z = jnp.where(iota8 == 2, cross, tail)
                    z = jnp.where(iota8 == 0, high, jnp.where(iota8 == 1, negative - high, z))
                    hats.append(jnp.concatenate([z, jnp.zeros((8, LANES), jnp.float32)], axis=0).astype(BF))
                    right.append(jnp.concatenate(hats, axis=0))
                pltpu.matmul_push_rhs(
                    jnp.concatenate(left, axis=1), staging_register=0, mxu_index=s % 2, transpose=True
                )
                pltpu.matmul_acc_lhs(accs[s], jnp.concatenate(right, axis=1), load_staged_rhs=0)

        def both(chunk, buf, ahead, other):
            pairs, groups = KT // 2, lines // 8
            done = 0
            for k2 in range(pairs):
                pair(buf, chunk, k2)
                while done < groups and done * pairs <= k2 * groups:
                    look(other, ahead, done)
                    done += 1

        for g in range(lines // 8):
            look(buf0, 0, g)

        def two(i, carry):
            both(2 * i, buf0, 2 * i + 1, buf1)
            both(2 * i + 1, buf1, jnp.minimum(2 * i + 2, chunks - 1), buf0)
            return carry

        lax.fori_loop(0, chunks // 2, two, 0)

        stats, lane = [], lax.broadcasted_iota(jnp.int32, (GROUPS, LANES), 1)
        sums = [pltpu.matmul_pop(a) for a in accs]
        for out in sums:
            stats.append(out[LANES:])
        stats.append(jnp.zeros((LANES - 16 * series, nblk * GROUPS), jnp.float32))
        turned = jnp.concatenate(stats, axis=0).T
        total = sum(turned[h * GROUPS:(h + 1) * GROUPS] for h in range(nblk))
        sub8 = lax.broadcasted_iota(jnp.int32, (8, LANES), 0)
        chunk_rows = out_ref.shape[0] // n
        hist_rows = own * series * nblk
        for s in range(series):
            c, m = divmod(s, 2)
            low = jnp.min(jnp.where(sub8 % C == c, low_ref[m], jnp.inf), keepdims=True)
            total = jnp.where(lane == 16 * series + s, low, total)
            full = sums[s][:LANES].T
            for h in range(nblk):
                value = full[h * GROUPS:(h + 1) * GROUPS]
                if h:
                    column = turned[(h - 1) * GROUPS:h * GROUPS, 16 * s + 2:16 * s + 3]
                    value = jnp.where(lane == 0, value + column, value)
                for i in range(n):
                    at = i * chunk_rows + (c * nblk + h) * 2 + m
                    out_ref[pl.ds(at, own, stride=series * nblk), :] = value[i * own:(i + 1) * own]
        for i in range(n):
            at = i * chunk_rows + hist_rows
            out_ref[at:at + own, :] = total[i * own:(i + 1) * own]

    pl.run_scoped(body, *[pltpu.ACC(s % 2)((LANES + 16, 256), jnp.float32) for s in range(series)])


def run_hist(edges, coarse, fine, ids, a, b, c, d, low, C, n, KT=16):
    nblk = fine.shape[0]
    own = GROUPS // n
    rows = own * 2 * C * nblk + own + (-own % 8)
    vm = pl.BlockSpec(memory_space=pltpu.VMEM)
    return pl.pallas_call(
        functools.partial(hist_kernel, C, KT, n),
        in_specs=[pl.BlockSpec(memory_space=pltpu.SMEM)] + [vm] * 8,
        out_shape=jax.ShapeDtypeStruct((n * rows, LANES), jnp.float32),
        scratch_shapes=[pltpu.VMEM((6, 2, KT * C, LANES), jnp.float32) for _ in range(2)],
        cost_estimate=pl.CostEstimate(
            flops=4 * C * (LANES + 16) * 256 * ids.size, bytes_accessed=16 * a.size, transcendentals=2 * a.size
        ),
        name="hist",
    )(edges, coarse, fine, ids, a, b, c, d, low)


def small_kernel(C, share, scale, stats_ref, part_ref, share_ref, tns_ref, wns_ref):
    turned = stats_ref[...].T
    tns = jnp.zeros((C, 2), jnp.float32)
    wns = jnp.zeros((C, 2), jnp.float32)
    row = lax.broadcasted_iota(jnp.int32, (C, 2), 0)
    col = lax.broadcasted_iota(jnp.int32, (C, 2), 1)
    for s in range(2 * C):
        c, m = divmod(s, 2)
        sums = turned[16 * s:16 * s + 1, :] + turned[16 * s + 1:16 * s + 2, :]
        part_ref[c, m:m + 1, :] = sums * share
        here = (row == c) & (col == m)
        tns = jnp.where(here, jnp.sum(sums, keepdims=True) * scale, tns)
        wns = jnp.where(here, turned[32 * C + s:32 * C + s + 1, :1], wns)
    share_ref[...] = turned[3:4, :] * share
    tns_ref[...] = tns
    wns_ref[...] = wns


def run_small(stats, C, endpoints):
    return pl.pallas_call(
        functools.partial(small_kernel, C, GROUPS / endpoints, 1.0 / endpoints),
        out_shape=[
            jax.ShapeDtypeStruct((C, 2, GROUPS), jnp.float32),
            jax.ShapeDtypeStruct((1, GROUPS), jnp.float32),
            jax.ShapeDtypeStruct((C, 2), jnp.float32),
            jax.ShapeDtypeStruct((C, 2), jnp.float32),
        ],
        name="small",
    )(stats)


def rotate(value, axis, distance):
    size = lax.axis_size(axis)
    return lax.ppermute(value, axis, [(i, (i + distance) % size) for i in range(size)])


def tiles(x):
    c, e = x.shape
    return x.reshape(c, e // LANES, LANES).transpose(1, 0, 2).reshape(-1, LANES)


def on_device(required, arrival, hold_required, early_arrival, part_ids, bin_edges):
    C, rows = required.shape
    bins = bin_edges.shape[0]
    n = lax.axis_size("ep")
    me = lax.axis_index("ep")
    endpoints = rows * n
    density = GROUPS * bins / endpoints
    series = 2 * C
    data = (tiles(required), tiles(arrival), tiles(early_arrival), tiles(hold_required))
    coarse, fine, near, low = run_prep(bin_edges, *data, C)
    shares = [rotate(near, "corner", d) for d in range(1, lax.axis_size("corner"))]
    chunks = run_hist(bin_edges, coarse, fine, part_ids.reshape(-1, LANES), *data, low, C, n)
    worst = functools.reduce(jnp.minimum, shares, near).reshape(rows // LANES, C, LANES)[:, :2]
    worst = worst.transpose(1, 0, 2).reshape(2, rows)

    own = GROUPS // n
    hrows = own * series * (bins // LANES)
    chunks = chunks.reshape(n, -1, LANES)
    total = lax.dynamic_index_in_dim(chunks, me, 0, False)
    lanes = lax.broadcasted_iota(jnp.int32, total[hrows:].shape, 1)
    hsum, ssum = total[:hrows], total[hrows:]
    for d in range(1, n):
        got = rotate(lax.dynamic_index_in_dim(chunks, (me + d) % n, 0, False), "ep", d)
        hsum = hsum + got[:hrows]
        ssum = jnp.where(lanes >= 16 * series, jnp.minimum(ssum, got[hrows:]), ssum + got[hrows:])
    mine = jnp.concatenate([hsum * density, ssum], axis=0)
    full = jnp.zeros((n, hrows, LANES), jnp.float32)
    sfull = jnp.zeros((n,) + ssum.shape, jnp.float32)
    for d in range(n):
        got = rotate(mine, "ep", d) if d else mine
        full = lax.dynamic_update_index_in_dim(full, got[:hrows], (me - d) % n, 0)
        sfull = lax.dynamic_update_index_in_dim(sfull, got[hrows:], (me - d) % n, 0)
    part_hist = (
        full.reshape(GROUPS, C, bins // LANES, 2, LANES).transpose(0, 1, 3, 2, 4).reshape(GROUPS, C, 2, bins)
    )
    stats = sfull[:, :own].reshape(GROUPS, LANES)
    part_tns, part_share, tns, wns = run_small(stats, C, endpoints)
    part_tns = part_tns.transpose(2, 0, 1)
    part_share = part_share.reshape(GROUPS)
    return (part_hist, part_tns, part_share, tns, wns, worst)


def solution(mesh):
    in_specs = (
        P("corner", "ep"),
        P("corner", "ep"),
        P("corner", "ep"),
        P("corner", "ep"),
        P("ep"),
        P(),
    )
    out_specs = (
        P(None, "corner", None, None),
        P(None, "corner", None),
        P(),
        P("corner", None),
        P("corner", None),
        P(None, "ep"),
    )
    return jax.shard_map(
        on_device, mesh=mesh, in_specs=in_specs, out_specs=out_specs, check_vma=False
    )
```

time: 187 us -> 69.3 us (0.37)
  matrix products: 68.7 us -> 0 us
  blocking collectives: 40.7 us -> 0 us
  Pallas kernels: 0 us -> 18.1 us
  other arithmetic: 17.8 us -> 2.48 us
  starting transfers between devices: 0.08 us -> 14.5 us
  between operations: 14.8 us -> 0.93 us
  local copies, waits for them, and re-layouts: 13.1 us -> 1.89 us
    dot_general x16 -> x0, matrix products: 68.7 us -> none  [the longest x8 63.7 us: one_block(): jnp.einsum('pe,kbe->pkb', member_low, weight, preferred_element_type=jnp....]
    ppermute x0 -> x17, waiting for transfers between devices: none -> 31.1 us  [rotate(): lax.ppermute(value, axis, [(i, (i + distance) % size) for i in range(size)])]
    psum x1 -> x0, waiting for transfers between devices: 30.8 us -> none  [on_device(): hist, stats, counts = lax.psum((hist, stats, counts), 'ep')]
    pmin x1 -> x0, blocking collectives: 23.5 us -> none  [on_device(): wns = lax.pmin(local_min, 'ep')]
    pallas_call x0 -> x3, Pallas kernels: none -> 18.1 us  [the longest x1 13.4 us: run_hist(): pl.pallas_call(functools.partial(hist_kernel, C, KT, n), in_specs=[pl.Blo...]
    psum x1 -> x0, blocking collectives: 17.2 us -> none  [on_device(): hist, stats, counts = lax.psum((hist, stats, counts), 'ep')]
    ppermute x0 -> x17, starting transfers between devices: none -> 14.5 us  [rotate(): lax.ppermute(value, axis, [(i, (i + distance) % size) for i in range(size)])]
    dynamic_slice x8 -> x0, local copies, waits for them, and re-layouts: 5.75 us -> none  [one_block(): ids_block = lax.dynamic_slice_in_dim(part_ids, start, block, 0)]
  transfers between devices with their start and end apart: 2 -> 17, of which waited for: 1 -> 7; matrix products, arithmetic and copies ran while one was open for 51% -> 0% of each run, Pallas kernels for 0% -> 2%
where the time goes in v1:
time: 69.3 us; the launch traced here: 69 us
  waiting for transfers between devices  31.1 us (45%)
  Pallas kernels  18.1 us (26%)
  starting transfers between devices  14.5 us (21%)
  other arithmetic  2.48 us (4%)
  local copies, waits for them, and re-layouts  1.89 us (3%)
  between operations  0.93 us (1%)
    ppermute x17, waiting for transfers between devices, rotate(): lax.ppermute(value, axis, [(i, (i + distance) % size) for i in range(size)])  31.1 us
    ppermute x17, starting transfers between devices, rotate(): lax.ppermute(value, axis, [(i, (i + distance) % size) for i in range(size)])  14.5 us
    pallas_call x1, Pallas kernels, run_hist(): pl.pallas_call(functools.partial(hist_kernel, C, KT, n), in_specs=[pl.Blo...  13.4 us
    pallas_call x1, Pallas kernels, run_prep(): pl.pallas_call(functools.partial(prep_kernel, C), in_specs=[pl.BlockSpec(...  3.14 us
    pallas_call x1, Pallas kernels, run_small(): pl.pallas_call(functools.partial(small_kernel, C, GROUPS / endpoints, 1.0...  1.52 us
  transfers between devices with their start and end apart: 17, of which 7 were waited for; matrix products, arithmetic and copies ran while one was open for 0% of the time, Pallas kernels for 2%

profile of v1, /device:TPU:0, one launch (start us, length us, event | category | flops | bytes accessed | tf_op | source)
XLA Modules:
  0.0 69.0 jit_solution(11097054868020649734)
XLA Ops:
  0.7 3.1 %prep.1 = (s32[4,128]{1,0:T(4,128)}, s32[4,128]{1,0:T(4,128)}, f32[512,128]{1,0:T(8,128)}, f32[2,8,128]{2,1,0:T(8,128)}) custom-call(s32[512]{0:T(512)} %edges_ref.3, s32[4,128]{1,0:T(4,128)} %bitcast.134, f32[512,128]{1,0:T(8,128)} %bitcast.125, f32[512,128]{1,0:T(8,128)} %bitcast.127, f32[512,128]{1,0:T(8,128)} %bitcast.129, f32[512,128]{1,0:T(8,128)} %bitcast.131), custom_call_target="tpu_custom_call" | custom-call | tf_op jit(solution)/shard_map/prep/pallas_call | solution.py:105
  3.9 13.4 %hist.1 = f32[1088,128]{1,0:T(8,128)} custom-call(s32[512]{0:T(512)} %edges_ref.3, s32[4,128]{1,0:T(4,128)} %get-tuple-element.14.coarse_ref, s32[4,128]{1,0:T(4,128)} %get-tuple-element.15.fine_ref, s32[256,128]{1,0:T(8,128)} %bitcast.135, f32[512,128]{1,0:T(8,128)} %bitcast.126, f32[512,128]{1,0:T(8,128)} %bitcast.128, f32[512,128]{1,0:T(8,128)} %bitcast.130, ...), custom_call_target="tpu_custom_call" | custom-call | flops 9663676416 | bytes 1048576 | tf_op jit(solution)/shard_map/hist/pallas_call | solution.py:235
  17.3 1.1 %dynamic-slice_bitcast_fusion.6 = (f32[136,128]{1,0:T(8,128)S(1)}, f32[136,128]{1,0:T(8,128)S(1)}, f32[136,128]{1,0:T(8,128)S(1)}, f32[136,128]{1,0:T(8,128)S(1)...) fusion(f32[8,136,128]{2,1,0:T(8,128)} %bitcast.120, s32[]{:T(128)S(6)} %select_n.162, ...), kind=kLoop, calls=%fused_computation.8 | loop fusion | bytes 974876 | tf_op jit(solution)/shard_map/jit(dynamic_index_in_dim)/squeeze | solution.py:310
  18.4 6.1 %collective-permute-start.6 = (f32[136,128]{1,0:T(8,128)S(1)}, f32[136,128]{1,0:T(8,128)S(1)}, u32[]{:S(2)}, u32[]{:S(2)}) collective-permute-start(f32[136,128]{1,0:T(8,128)S(1)} %get-tuple-element.27), channel_id=1, source_target_pairs={{0,28},{4,0},{8,4},{12,8},{16,12},{20,16},{24,20},{28,24},{1,29},{... | collective-permute-start | bytes 208904 | tf_op jit(solution)/shard_map/ppermute | solution.py:280
  24.5 0.5 collective-permute-start.5
  24.9 0.0 collective-permute-start.4
  24.9 3.0 %collective-permute-start.3 = (f32[136,128]{1,0:T(8,128)S(1)}, f32[136,128]{1,0:T(8,128)S(1)}, u32[]{:S(2)}, u32[]{:S(2)}) collective-permute-start(f32[136,128]{1,0:T(8,128)S(1)} %get-tuple-element.30), channel_id=1, source_target_pairs={{0,16},{4,20},{8,24},{12,28},{16,0},{20,4},{24,8},{28,12},{1,17},{... | collective-permute-start | bytes 208904 | tf_op jit(solution)/shard_map/ppermute | solution.py:280
  27.9 0.0 collective-permute-start.2
  27.9 0.0 collective-permute-done.6
  27.9 1.8 %collective-permute-start.1 = (f32[136,128]{1,0:T(8,128)S(1)}, f32[136,128]{1,0:T(8,128)S(1)}, u32[]{:S(2)}, u32[]{:S(2)}) collective-permute-start(f32[136,128]{1,0:T(8,128)S(1)} %get-tuple-element.32), channel_id=1, source_target_pairs={{0,8},{4,12},{8,16},{12,20},{16,24},{20,28},{24,0},{28,4},{1,9},{5... | collective-permute-start | bytes 208904 | tf_op jit(solution)/shard_map/ppermute | solution.py:280
  29.8 0.0 collective-permute-done.5
  29.8 1.1 %collective-permute-start = (f32[136,128]{1,0:T(8,128)S(1)}, f32[136,128]{1,0:T(8,128)S(1)}, u32[]{:S(2)}, u32[]{:S(2)}) collective-permute-start(f32[136,128]{1,0:T(8,128)S(1)} %get-tuple-element.26), channel_id=1, source_target_pairs={{0,4},{4,8},{8,12},{12,16},{16,20},{20,24},{24,28},{28,0},{1,5},{5... | collective-permute-start | bytes 208904 | tf_op jit(solution)/shard_map/ppermute | solution.py:280
  30.9 0.0 collective-permute-done.4
  30.9 5.5 %collective-permute-done.3 = f32[136,128]{1,0:T(8,128)S(1)} collective-permute-done((f32[136,128]{1,0:T(8,128)S(1)}, f32[136,128]{1,0:T(8,128)S(1)}, u32[]{:S(2)}, u32[]{:S(2)}) %collective-permute-start.3) | collective-permute-done | bytes 69664 | tf_op jit(solution)/shard_map/ppermute | solution.py:280
  36.4 2.7 %collective-permute-done.2 = f32[136,128]{1,0:T(8,128)S(1)} collective-permute-done((f32[136,128]{1,0:T(8,128)S(1)}, f32[136,128]{1,0:T(8,128)S(1)}, u32[]{:S(2)}, u32[]{:S(2)}) %collective-permute-start.2) | collective-permute-done | bytes 69664 | tf_op jit(solution)/shard_map/ppermute | solution.py:280
  39.1 0.0 collective-permute-done.1
  39.1 0.0 collective-permute-done
  39.2 0.0 copy-start.1
  39.2 0.9 %bitcast_dynamic-update-slice_fusion = (f32[8,128,128]{2,1,0:T(8,128)S(1)}, f32[128,128]{1,0:T(8,128)S(1)}) fusion(f32[8,128,128]{2,1,0:T(8,128)S(1)} %broadcast_in_dim.56, s32[]{:T(128)S(6)} %select_n.176, f32[136,128]{1,0:T(8,128)S(1)} %collective-permute-done.6, f32[136,128]{1,0:T(8,128)S(1)} %collective-permute-done.5, ...), kind=kLoop, calls=%fused_computation.32 | loop fusion | flops 131072 | bytes 655368 | tf_op jit(solution)/shard_map/jit(dynamic_update_index_in_dim)/dynamic_update_slice | solution.py:318
  40.1 0.7 %constant_dynamic-update-slice_fusion.7 = (f32[8,8,128]{2,1,0:T(8,128)S(1)}, f32[8,128]{1,0:T(8,128)S(1)}) fusion(f32[8,8,128]{2,1,0:T(8,128)S(1)} %broadcast_in_dim.65, s32[]{:T(128)S(6)} %select_n.176, f32[136,128]{1,0:T(8,128)S(1)} %collective-permute-done.6, f32[136,128]{1,0:T(8,128)S(1)} %collective-permute-done.5, ...), kind=kLoop, calls=%fused_computation.40 | loop fusion | flops 21504 | bytes 41484 | tf_op jit(solution)/shard_map/jit(dynamic_update_index_in_dim)/dynamic_update_slice | solution.py:319
  40.9 0.1 collective-permute-start.7
  40.9 0.0 copy-done.1
  40.9 0.1 collective-permute-start.16
  41.0 1.6 %collective-permute-start.15 = (f32[512,128]{1,0:T(8,128)S(1)}, f32[512,128]{1,0:T(8,128)S(1)}, u32[]{:S(2)}, u32[]{:S(2)}) collective-permute-start(f32[512,128]{1,0:T(8,128)S(1)} %copy-done.1), channel_id=1, source_target_pairs={{0,2},{1,3},{2,0},{3,1},{4,6},{5,7},{6,4},{7,5},{8,10},{9,11},{10,... | collective-permute-start | bytes 786440 | tf_op jit(solution)/shard_map/ppermute | solution.py:280
  42.6 0.2 collective-permute-start.14
  42.7 0.0 collective-permute-start.8
  42.7 5.2 %collective-permute-done.7 = f32[136,128]{1,0:T(8,128)S(1)} collective-permute-done((f32[136,128]{1,0:T(8,128)S(1)}, f32[136,128]{1,0:T(8,128)S(1)}, u32[]{:S(2)}, u32[]{:S(2)}) %collective-permute-start.7) | collective-permute-done | bytes 69664 | tf_op jit(solution)/shard_map/ppermute | solution.py:280
  47.9 0.0 collective-permute-start.9
  48.0 1.1 %collective-permute-done.8 = f32[136,128]{1,0:T(8,128)S(1)} collective-permute-done((f32[136,128]{1,0:T(8,128)S(1)}, f32[136,128]{1,0:T(8,128)S(1)}, u32[]{:S(2)}, u32[]{:S(2)}) %collective-permute-start.8) | collective-permute-done | bytes 69664 | tf_op jit(solution)/shard_map/ppermute | solution.py:280
  49.1 0.0 collective-permute-start.10
  49.1 7.2 %collective-permute-done.9 = f32[136,128]{1,0:T(8,128)S(1)} collective-permute-done((f32[136,128]{1,0:T(8,128)S(1)}, f32[136,128]{1,0:T(8,128)S(1)}, u32[]{:S(2)}, u32[]{:S(2)}) %collective-permute-start.9) | collective-permute-done | bytes 69664 | tf_op jit(solution)/shard_map/ppermute | solution.py:280
  56.3 0.0 collective-permute-start.11
  56.3 0.0 collective-permute-done.10
  56.3 0.1 collective-permute-start.12
  56.5 5.1 %collective-permute-done.11 = f32[136,128]{1,0:T(8,128)S(1)} collective-permute-done((f32[136,128]{1,0:T(8,128)S(1)}, f32[136,128]{1,0:T(8,128)S(1)}, u32[]{:S(2)}, u32[]{:S(2)}) %collective-permute-start.11) | collective-permute-done | bytes 69664 | tf_op jit(solution)/shard_map/ppermute | solution.py:280
  61.6 0.0 collective-permute-start.13
  61.6 0.0 collective-permute-done.12
  61.7 4.2 %collective-permute-done.13 = f32[136,128]{1,0:T(8,128)S(1)} collective-permute-done((f32[136,128]{1,0:T(8,128)S(1)}, f32[136,128]{1,0:T(8,128)S(1)}, u32[]{:S(2)}, u32[]{:S(2)}) %collective-permute-start.13) | collective-permute-done | bytes 69664 | tf_op jit(solution)/shard_map/ppermute | solution.py:280
  65.9 0.0 copy-start.2
  65.9 0.6 copy-done.2
  66.5 1.5 %small.1 = (f32[2,2,64]{2,1,0:T(2,128)}, f32[1,64]{1,0:T(1,128)}, f32[2,2]{1,0:T(2,128)}, f32[2,2]{1,0:T(2,128)}) custom-call(f32[64,128]{1,0:T(8,128)} %bitcast.133), custom_call_target="tpu_custom_call" | custom-call | tf_op jit(solution)/shard_map/small/pallas_call | solution.py:266
  68.1 0.0 copy-start
  68.1 0.0 collective-permute-done.16
  68.1 0.0 collective-permute-done.15
  68.1 0.0 collective-permute-done.14
  68.1 0.8 %minimum_minimum_fusion = f32[512,128]{1,0:T(8,128)} fusion(f32[512,128]{1,0:T(8,128)S(1)} %collective-permute-done.16, f32[512,128]{1,0:T(8,128)S(1)} %collective-permute-done.15, f32[512,128]{1,0:T(8,128)S(1)} %copy-done.1, f32[512,128]{1,0:T(8,128)S(1)} %collective-permute-done.14), kind=kLoop, calls=%fused_computation | loop fusion | flops 196608 | bytes 1310720 | tf_op jit(solution)/shard_map/min | solution.py:300
  69.0 0.0 copy-done
  (18 shorter events, 0.2 us)
Async XLA Ops:
  18.4 9.5 %collective-permute-start.6 = (f32[136,128]{1,0:T(8,128)S(1)}, f32[136,128]{1,0:T(8,128)S(1)}, u32[]{:S(2)}, u32[]{:S(2)}) collective-permute-start(f32[136,128]{1,0:T(8,128)S(1)} %get-tuple-element.27), channel_id=1, source_target_pairs={{0,28},{4,0},{8,4},{12,8},{16,12},{20,16},{24,20},{28,24},{1,29},{... | collective-permute-start | bytes 208904 | tf_op jit(solution)/shard_map/ppermute | solution.py:280
  24.5 5.3 %collective-permute-start.5 = (f32[136,128]{1,0:T(8,128)S(1)}, f32[136,128]{1,0:T(8,128)S(1)}, u32[]{:S(2)}, u32[]{:S(2)}) collective-permute-start(f32[136,128]{1,0:T(8,128)S(1)} %get-tuple-element.28), channel_id=1, source_target_pairs={{0,24},{4,28},{8,0},{12,4},{16,8},{20,12},{24,16},{28,20},{1,25},{... | collective-permute-start | bytes 208904 | tf_op jit(solution)/shard_map/ppermute | solution.py:280
  24.9 6.0 %collective-permute-start.4 = (f32[136,128]{1,0:T(8,128)S(1)}, f32[136,128]{1,0:T(8,128)S(1)}, u32[]{:S(2)}, u32[]{:S(2)}) collective-permute-start(f32[136,128]{1,0:T(8,128)S(1)} %get-tuple-element.29), channel_id=1, source_target_pairs={{0,20},{4,24},{8,28},{12,0},{16,4},{20,8},{24,12},{28,16},{1,21},{... | collective-permute-start | bytes 208904 | tf_op jit(solution)/shard_map/ppermute | solution.py:280
  24.9 11.5 %collective-permute-start.3 = (f32[136,128]{1,0:T(8,128)S(1)}, f32[136,128]{1,0:T(8,128)S(1)}, u32[]{:S(2)}, u32[]{:S(2)}) collective-permute-start(f32[136,128]{1,0:T(8,128)S(1)} %get-tuple-element.30), channel_id=1, source_target_pairs={{0,16},{4,20},{8,24},{12,28},{16,0},{20,4},{24,8},{28,12},{1,17},{... | collective-permute-start | bytes 208904 | tf_op jit(solution)/shard_map/ppermute | solution.py:280
  27.9 11.2 %collective-permute-start.2 = (f32[136,128]{1,0:T(8,128)S(1)}, f32[136,128]{1,0:T(8,128)S(1)}, u32[]{:S(2)}, u32[]{:S(2)}) collective-permute-start(f32[136,128]{1,0:T(8,128)S(1)} %get-tuple-element.31), channel_id=1, source_target_pairs={{0,12},{4,16},{8,20},{12,24},{16,28},{20,0},{24,4},{28,8},{1,13},{... | collective-permute-start | bytes 208904 | tf_op jit(solution)/shard_map/ppermute | solution.py:280
  27.9 11.2 %collective-permute-start.1 = (f32[136,128]{1,0:T(8,128)S(1)}, f32[136,128]{1,0:T(8,128)S(1)}, u32[]{:S(2)}, u32[]{:S(2)}) collective-permute-start(f32[136,128]{1,0:T(8,128)S(1)} %get-tuple-element.32), channel_id=1, source_target_pairs={{0,8},{4,12},{8,16},{12,20},{16,24},{20,28},{24,0},{28,4},{1,9},{5... | collective-permute-start | bytes 208904 | tf_op jit(solution)/shard_map/ppermute | solution.py:280
  29.8 9.4 %collective-permute-start = (f32[136,128]{1,0:T(8,128)S(1)}, f32[136,128]{1,0:T(8,128)S(1)}, u32[]{:S(2)}, u32[]{:S(2)}) collective-permute-start(f32[136,128]{1,0:T(8,128)S(1)} %get-tuple-element.26), channel_id=1, source_target_pairs={{0,4},{4,8},{8,12},{12,16},{16,20},{20,24},{24,28},{28,0},{1,5},{5... | collective-permute-start | bytes 208904 | tf_op jit(solution)/shard_map/ppermute | solution.py:280
  39.2 1.7 %copy-start.1 = (f32[512,128]{1,0:T(8,128)S(1)}, f32[512,128]{1,0:T(8,128)}, u32[]{:S(2)}) copy-start(f32[512,128]{1,0:T(8,128)} %get-tuple-element.21) | copy-start | bytes 786436
  40.9 7.1 %collective-permute-start.7 = (f32[136,128]{1,0:T(8,128)S(1)}, f32[136,128]{1,0:T(8,128)S(1)}, u32[]{:S(2)}, u32[]{:S(2)}) collective-permute-start(f32[136,128]{1,0:T(8,128)S(1)} %pad_maximum_fusion), channel_id=1, source_target_pairs={{0,4},{4,8},{8,12},{12,16},{16,20},{20,24},{24,28},{28,0},{1,5},{5... | collective-permute-start | bytes 208904 | tf_op jit(solution)/shard_map/ppermute | solution.py:280
  40.9 27.2 %collective-permute-start.16 = (f32[512,128]{1,0:T(8,128)S(1)}, f32[512,128]{1,0:T(8,128)S(1)}, u32[]{:S(2)}, u32[]{:S(2)}) collective-permute-start(f32[512,128]{1,0:T(8,128)S(1)} %copy-done.1), channel_id=1, source_target_pairs={{0,3},{1,0},{2,1},{3,2},{4,7},{5,4},{6,5},{7,6},{8,11},{9,8},{10,9... | collective-permute-start | bytes 786440 | tf_op jit(solution)/shard_map/ppermute | solution.py:280
  41.0 27.1 %collective-permute-start.15 = (f32[512,128]{1,0:T(8,128)S(1)}, f32[512,128]{1,0:T(8,128)S(1)}, u32[]{:S(2)}, u32[]{:S(2)}) collective-permute-start(f32[512,128]{1,0:T(8,128)S(1)} %copy-done.1), channel_id=1, source_target_pairs={{0,2},{1,3},{2,0},{3,1},{4,6},{5,7},{6,4},{7,5},{8,10},{9,11},{10,... | collective-permute-start | bytes 786440 | tf_op jit(solution)/shard_map/ppermute | solution.py:280
  42.6 25.5 %collective-permute-start.14 = (f32[512,128]{1,0:T(8,128)S(1)}, f32[512,128]{1,0:T(8,128)S(1)}, u32[]{:S(2)}, u32[]{:S(2)}) collective-permute-start(f32[512,128]{1,0:T(8,128)S(1)} %copy-done.1), channel_id=1, source_target_pairs={{0,1},{1,2},{2,3},{3,0},{4,5},{5,6},{6,7},{7,4},{8,9},{9,10},{10,1... | collective-permute-start | bytes 786440 | tf_op jit(solution)/shard_map/ppermute | solution.py:280
  42.7 6.4 %collective-permute-start.8 = (f32[136,128]{1,0:T(8,128)S(1)}, f32[136,128]{1,0:T(8,128)S(1)}, u32[]{:S(2)}, u32[]{:S(2)}) collective-permute-start(f32[136,128]{1,0:T(8,128)S(1)} %pad_maximum_fusion), channel_id=1, source_target_pairs={{0,8},{4,12},{8,16},{12,20},{16,24},{20,28},{24,0},{28,4},{1,9},{5... | collective-permute-start | bytes 208904 | tf_op jit(solution)/shard_map/ppermute | solution.py:280
  47.9 8.4 %collective-permute-start.9 = (f32[136,128]{1,0:T(8,128)S(1)}, f32[136,128]{1,0:T(8,128)S(1)}, u32[]{:S(2)}, u32[]{:S(2)}) collective-permute-start(f32[136,128]{1,0:T(8,128)S(1)} %pad_maximum_fusion), channel_id=1, source_target_pairs={{0,12},{4,16},{8,20},{12,24},{16,28},{20,0},{24,4},{28,8},{1,13},{... | collective-permute-start | bytes 208904 | tf_op jit(solution)/shard_map/ppermute | solution.py:280
  49.1 7.2 %collective-permute-start.10 = (f32[136,128]{1,0:T(8,128)S(1)}, f32[136,128]{1,0:T(8,128)S(1)}, u32[]{:S(2)}, u32[]{:S(2)}) collective-permute-start(f32[136,128]{1,0:T(8,128)S(1)} %pad_maximum_fusion), channel_id=1, source_target_pairs={{0,16},{4,20},{8,24},{12,28},{16,0},{20,4},{24,8},{28,12},{1,17},{... | collective-permute-start | bytes 208904 | tf_op jit(solution)/shard_map/ppermute | solution.py:280
  56.3 5.3 %collective-permute-start.11 = (f32[136,128]{1,0:T(8,128)S(1)}, f32[136,128]{1,0:T(8,128)S(1)}, u32[]{:S(2)}, u32[]{:S(2)}) collective-permute-start(f32[136,128]{1,0:T(8,128)S(1)} %pad_maximum_fusion), channel_id=1, source_target_pairs={{0,20},{4,24},{8,28},{12,0},{16,4},{20,8},{24,12},{28,16},{1,21},{... | collective-permute-start | bytes 208904 | tf_op jit(solution)/shard_map/ppermute | solution.py:280
  56.3 5.3 %collective-permute-start.12 = (f32[136,128]{1,0:T(8,128)S(1)}, f32[136,128]{1,0:T(8,128)S(1)}, u32[]{:S(2)}, u32[]{:S(2)}) collective-permute-start(f32[136,128]{1,0:T(8,128)S(1)} %pad_maximum_fusion), channel_id=1, source_target_pairs={{0,24},{4,28},{8,0},{12,4},{16,8},{20,12},{24,16},{28,20},{1,25},{... | collective-permute-start | bytes 208904 | tf_op jit(solution)/shard_map/ppermute | solution.py:280
  61.6 4.3 %collective-permute-start.13 = (f32[136,128]{1,0:T(8,128)S(1)}, f32[136,128]{1,0:T(8,128)S(1)}, u32[]{:S(2)}, u32[]{:S(2)}) collective-permute-start(f32[136,128]{1,0:T(8,128)S(1)} %pad_maximum_fusion), channel_id=1, source_target_pairs={{0,28},{4,0},{8,4},{12,8},{16,12},{20,16},{24,20},{28,24},{1,29},{... | collective-permute-start | bytes 208904 | tf_op jit(solution)/shard_map/ppermute | solution.py:280
  65.9 0.6 copy-start.2
  68.1 0.9 %copy-start = (f32[8,128,128]{2,1,0:T(8,128)}, f32[8,128,128]{2,1,0:T(8,128)S(1)}, u32[]{:S(2)}) copy-start(f32[8,128,128]{2,1,0:T(8,128)S(1)} %fusion) | copy-start | bytes 1572868

commit v2 on v1

--- a/solution.py
+++ b/solution.py
@@ -55,7 +55,10 @@
     )
 
 
-def prep_kernel(C, edges_ref, lines_ref, a_ref, b_ref, c_ref, d_ref, coarse_ref, fine_ref, worst_ref, low_ref):
+def prep_kernel(
+    C, edges_ref, side_ref, lines_ref, ids_ref, a_ref, b_ref, c_ref, d_ref,
+    coarse_ref, fine_ref, worst_ref, keep_ref, send_ref,
+):
     bins = edges_ref.shape[0]
     cell = lax.broadcasted_iota(jnp.int32, coarse_ref.shape, 0) * LANES + lax.broadcasted_iota(
         jnp.int32, coarse_ref.shape, 1
@@ -83,44 +86,54 @@
     following = jnp.where(last, below, left)
     fine_ref[...] = q + (following - q) * 65536
 
-    setup = a_ref[...] - b_ref[...]
-    hold = c_ref[...] - d_ref[...]
-    size = setup.shape[0]
-    for m, slack in enumerate((setup, hold)):
-        low_ref[m] = jnp.min(slack.reshape(size // 8, 8, LANES), axis=0)
-    first = lax.broadcasted_iota(jnp.int32, setup.shape, 0) % C == 0
-    for m, slack in enumerate((setup, hold)):
-        least = slack
-        for c in range(1, C):
-            least = jnp.minimum(least, pltpu.roll(slack, size - c, 0))
-        if m:
-            least = pltpu.roll(least, 1, 0)
-            worst_ref[...] = jnp.where(first, worst_ref[...], least)
-        else:
-            worst_ref[...] = least
-
-
-def run_prep(edges, a, b, c, d, C):
+    flag = side_ref[0] == 0
+    half = C // 2
+    lines = a_ref.shape[0] // C
+    for m, (late, early) in enumerate(((a_ref, b_ref), (c_ref, d_ref))):
+        for k in range(half):
+            pieces = []
+            for c in (k, k + half):
+                at = pl.ds(c, lines, stride=C)
+                pieces.append(late[at, :] - early[at, :])
+            keep_ref[m, pl.ds(k, lines, stride=half), :] = jnp.where(flag, pieces[0], pieces[1])
+            send_ref[m, pl.ds(k, lines, stride=half), :] = jnp.where(flag, pieces[1], pieces[0])
+            for piece in pieces:
+                first = k == 0 and piece is pieces[0]
+                at = pl.ds(m, lines, stride=2)
+                worst_ref[at, :] = piece if first else jnp.minimum(worst_ref[at, :], piece)
+    ids = ids_ref[...].astype(jnp.float32)
+    keep_ref[2, :lines, :] = ids
+    send_ref[2, :lines, :] = ids
+
+
+def run_prep(edges, side, ids, a, b, c, d, C):
     bins = edges.shape[0]
+    lines = ids.shape[0]
+    smem = pl.BlockSpec(memory_space=pltpu.SMEM)
     return pl.pallas_call(
         functools.partial(prep_kernel, C),
-        in_specs=[pl.BlockSpec(memory_space=pltpu.SMEM)] + [pl.BlockSpec(memory_space=pltpu.VMEM)] * 5,
+        in_specs=[smem, smem] + [pl.BlockSpec(memory_space=pltpu.VMEM)] * 6,
         out_shape=[
             jax.ShapeDtypeStruct((LEAST // 8 // LANES, LANES), jnp.int32),
             jax.ShapeDtypeStruct((bins // LANES, LANES), jnp.int32),
-            jax.ShapeDtypeStruct(a.shape, jnp.float32),
-            jax.ShapeDtypeStruct((2, 8, LANES), jnp.float32),
+            jax.ShapeDtypeStruct((2 * lines, LANES), jnp.float32),
+            jax.ShapeDtypeStruct((3, lines * C // 2, LANES), jnp.float32),
+            jax.ShapeDtypeStruct((3, lines * C // 2, LANES), jnp.float32),
         ],
         name="prep",
-    )(edges, edges.reshape(-1, LANES), a, b, c, d)
-
-
-def hist_kernel(C, KT, n, edges_ref, coarse_ref, fine_ref, ids_ref, a_ref, b_ref, c_ref, d_ref, low_ref, out_ref, buf0, buf1):
+    )(edges, side, edges.reshape(-1, LANES), ids, a, b, c, d)
+
+
+def hist_kernel(C, KT, n, edges_ref, place_ref, coarse_ref, fine_ref, slack_ref, *refs):
+    if n:
+        prior_ref, prior_low_ref = refs[:2]
+        outs, (low_ref, buf0, buf1, all_ref) = refs[2:2 + n], refs[2 + n:]
+    else:
+        out_ref, low_ref, buf0, buf1 = refs
     series = 2 * C
     nblk = fine_ref.shape[0]
     lines = KT * C
-    chunks = ids_ref.shape[0] // KT
-    own = GROUPS // n
+    chunks = slack_ref.shape[1] // lines
     x0 = edges_ref[0].astype(jnp.float32) * jnp.float32(STEP)
 
     def body(*accs):
@@ -144,14 +157,16 @@
         def look(buf, chunk, g):
             start = pl.multiple_of(chunk * lines + g * 8, 8)
             at = pl.ds(start, 8)
-            for m, slack in enumerate((a_ref[at, :] - b_ref[at, :], c_ref[at, :] - d_ref[at, :])):
+            for m in range(2):
+                slack = slack_ref[m, at, :]
+                low_ref[m] = jnp.minimum(low_ref[m], slack)
                 for i, v in enumerate(interval(slack, x0, coarse_ref, fine_ref)):
                     buf[i, m, g * 8:g * 8 + 8, :] = v
 
         def pair(buf, chunk, k2):
             member = []
             for kk in range(2):
-                ids = wide(ids_ref[pl.ds(chunk * KT + 2 * k2 + kk, 1), :], 32).astype(jnp.float32).astype(BF)
+                ids = wide(slack_ref[2, pl.ds(chunk * KT + 2 * k2 + kk, 1), :], 32).astype(BF)
                 member.append([jnp.where(i == ids, one, zero32).astype(F8) for i in iotas32])
             for s in range(series):
                 c, m = divmod(s, 2)
@@ -187,6 +202,7 @@
                     look(other, ahead, done)
                     done += 1
 
+        low_ref[...] = prior_low_ref[...] if n else jnp.full(low_ref.shape, jnp.inf)
         for g in range(lines // 8):
             look(buf0, 0, g)
 
@@ -199,13 +215,19 @@
 
         stats, lane = [], lax.broadcasted_iota(jnp.int32, (GROUPS, LANES), 1)
         sums = [pltpu.matmul_pop(a) for a in accs]
+        if not n:
+            for s in range(series):
+                out_ref[s] = sums[s]
+            return
+        sums = [prior_ref[s] + sums[s] for s in range(series)]
+        own = GROUPS // n
         for out in sums:
             stats.append(out[LANES:])
         stats.append(jnp.zeros((LANES - 16 * series, nblk * GROUPS), jnp.float32))
         turned = jnp.concatenate(stats, axis=0).T
         total = sum(turned[h * GROUPS:(h + 1) * GROUPS] for h in range(nblk))
         sub8 = lax.broadcasted_iota(jnp.int32, (8, LANES), 0)
-        chunk_rows = out_ref.shape[0] // n
+        chunk_rows = all_ref.shape[0] // n
         hist_rows = own * series * nblk
         for s in range(series):
             c, m = divmod(s, 2)
@@ -219,60 +241,90 @@
                     value = jnp.where(lane == 0, value + column, value)
                 for i in range(n):
                     at = i * chunk_rows + (c * nblk + h) * 2 + m
-                    out_ref[pl.ds(at, own, stride=series * nblk), :] = value[i * own:(i + 1) * own]
+                    all_ref[pl.ds(at, own, stride=series * nblk), :] = value[i * own:(i + 1) * own]
         for i in range(n):
             at = i * chunk_rows + hist_rows
-            out_ref[at:at + own, :] = total[i * own:(i + 1) * own]
+            all_ref[at:at + own, :] = total[i * own:(i + 1) * own]
+        for d in range(n):
+            at = pl.multiple_of(lax.rem(place_ref[0] + d, n) * chunk_rows, 8)
+            outs[d][...] = all_ref[pl.ds(at, chunk_rows), :]
 
     pl.run_scoped(body, *[pltpu.ACC(s % 2)((LANES + 16, 256), jnp.float32) for s in range(series)])
 
 
-def run_hist(edges, coarse, fine, ids, a, b, c, d, low, C, n, KT=16):
+def run_hist(edges, place, coarse, fine, slack, C, n=0, prior=(), KT=16):
     nblk = fine.shape[0]
-    own = GROUPS // n
-    rows = own * 2 * C * nblk + own + (-own % 8)
+    series = 2 * C
+    smem = pl.BlockSpec(memory_space=pltpu.SMEM)
     vm = pl.BlockSpec(memory_space=pltpu.VMEM)
+    scratch = [pltpu.VMEM((6, 2, KT * C, LANES), jnp.float32) for _ in range(2)]
+    low = jax.ShapeDtypeStruct((2, 8, LANES), jnp.float32)
+    if n:
+        own = GROUPS // n
+        rows = own * series * nblk + own + (-own % 8)
+        outs = [jax.ShapeDtypeStruct((rows, LANES), jnp.float32) for _ in range(n)]
+        scratch += [pltpu.VMEM((2, 8, LANES), jnp.float32)] * 0 + [pltpu.VMEM((n * rows, LANES), jnp.float32)]
+    else:
+        outs = [jax.ShapeDtypeStruct((series, LANES + 16, nblk * GROUPS), jnp.float32)]
     return pl.pallas_call(
         functools.partial(hist_kernel, C, KT, n),
-        in_specs=[pl.BlockSpec(memory_space=pltpu.SMEM)] + [vm] * 8,
-        out_shape=jax.ShapeDtypeStruct((n * rows, LANES), jnp.float32),
-        scratch_shapes=[pltpu.VMEM((6, 2, KT * C, LANES), jnp.float32) for _ in range(2)],
+        in_specs=[smem, smem] + [vm] * (3 + len(prior)),
+        out_shape=outs + [low],
+        scratch_shapes=scratch,
         cost_estimate=pl.CostEstimate(
-            flops=4 * C * (LANES + 16) * 256 * ids.size, bytes_accessed=16 * a.size, transcendentals=2 * a.size
+            flops=4 * (LANES + 16) * 256 * slack.size // 3, bytes_accessed=8 * slack.size, transcendentals=slack.size
         ),
         name="hist",
-    )(edges, coarse, fine, ids, a, b, c, d, low)
-
-
-def small_kernel(C, share, scale, stats_ref, part_ref, share_ref, tns_ref, wns_ref):
-    turned = stats_ref[...].T
+    )(edges, place, coarse, fine, slack, *prior)
+
+
+def final_kernel(C, own, share, scale, me_ref, *refs):
+    n = len(refs) - 6
+    pieces = refs[:n]
+    hist_ref, part_ref, share_ref, tns_ref, wns_ref, stats_ref = refs[n:]
+    half = C // 2
+    each = hist_ref.shape[0] // GROUPS // 2
+    for d in range(n):
+        source = lax.rem(me_ref[0] - d + n, n)
+        place, side = source >> 1, source & 1
+        for p in range(own):
+            at = pl.multiple_of((place * own + p) * 2 * each + side * each, 8)
+            hist_ref[pl.ds(at, each), :] = pieces[d][p * each:(p + 1) * each, :]
+        stats_ref[side, pl.ds(place * own, own), :] = pieces[d][own * each:own * each + own, :]
     tns = jnp.zeros((C, 2), jnp.float32)
     wns = jnp.zeros((C, 2), jnp.float32)
     row = lax.broadcasted_iota(jnp.int32, (C, 2), 0)
     col = lax.broadcasted_iota(jnp.int32, (C, 2), 1)
-    for s in range(2 * C):
-        c, m = divmod(s, 2)
-        sums = turned[16 * s:16 * s + 1, :] + turned[16 * s + 1:16 * s + 2, :]
-        part_ref[c, m:m + 1, :] = sums * share
-        here = (row == c) & (col == m)
-        tns = jnp.where(here, jnp.sum(sums, keepdims=True) * scale, tns)
-        wns = jnp.where(here, turned[32 * C + s:32 * C + s + 1, :1], wns)
+    for side in range(2):
+        turned = stats_ref[side].T
+        for s in range(2 * half):
+            c, m = divmod(s, 2)
+            c += side * half
+            sums = turned[16 * s:16 * s + 1, :] + turned[16 * s + 1:16 * s + 2, :]
+            part_ref[c, m:m + 1, :] = sums * share
+            here = (row == c) & (col == m)
+            tns = jnp.where(here, jnp.sum(sums, keepdims=True) * scale, tns)
+            wns = jnp.where(here, turned[32 * half + s:32 * half + s + 1, :1], wns)
     share_ref[...] = turned[3:4, :] * share
     tns_ref[...] = tns
     wns_ref[...] = wns
 
 
-def run_small(stats, C, endpoints):
+def run_final(me, pieces, C, own, rows, endpoints):
+    vm = pl.BlockSpec(memory_space=pltpu.VMEM)
     return pl.pallas_call(
-        functools.partial(small_kernel, C, GROUPS / endpoints, 1.0 / endpoints),
+        functools.partial(final_kernel, C, own, GROUPS / endpoints, 1.0 / endpoints),
+        in_specs=[pl.BlockSpec(memory_space=pltpu.SMEM)] + [vm] * len(pieces),
         out_shape=[
+            jax.ShapeDtypeStruct((GROUPS * rows, LANES), jnp.float32),
             jax.ShapeDtypeStruct((C, 2, GROUPS), jnp.float32),
             jax.ShapeDtypeStruct((1, GROUPS), jnp.float32),
             jax.ShapeDtypeStruct((C, 2), jnp.float32),
             jax.ShapeDtypeStruct((C, 2), jnp.float32),
         ],
-        name="small",
-    )(stats)
+        scratch_shapes=[pltpu.VMEM((2, GROUPS, LANES), jnp.float32)],
+        name="final",
+    )(me, *pieces)
 
 
 def rotate(value, axis, distance):
@@ -292,36 +344,36 @@
     me = lax.axis_index("ep")
     endpoints = rows * n
     density = GROUPS * bins / endpoints
-    series = 2 * C
+    half = C // 2
+    side = me % 2
+    place = me // 2
+    rest = n // 2
     data = (tiles(required), tiles(arrival), tiles(early_arrival), tiles(hold_required))
-    coarse, fine, near, low = run_prep(bin_edges, *data, C)
+    ids = part_ids.reshape(-1, LANES)
+    lines = ids.shape[0]
+    coarse, fine, near, keep, send = run_prep(bin_edges, side.reshape(1), ids, *data, C)
+    got = lax.ppermute(send, "ep", [(i, i ^ 1) for i in range(n)])
     shares = [rotate(near, "corner", d) for d in range(1, lax.axis_size("corner"))]
-    chunks = run_hist(bin_edges, coarse, fine, part_ids.reshape(-1, LANES), *data, low, C, n)
-    worst = functools.reduce(jnp.minimum, shares, near).reshape(rows // LANES, C, LANES)[:, :2]
+    prior = run_hist(bin_edges, place.reshape(1), coarse, fine, keep, half)
+    chunks = run_hist(bin_edges, place.reshape(1), coarse, fine, got, half, rest, prior)
+    worst = functools.reduce(jnp.minimum, shares, near).reshape(lines, 2, LANES)
     worst = worst.transpose(1, 0, 2).reshape(2, rows)
 
-    own = GROUPS // n
-    hrows = own * series * (bins // LANES)
-    chunks = chunks.reshape(n, -1, LANES)
-    total = lax.dynamic_index_in_dim(chunks, me, 0, False)
+    own = GROUPS // rest
+    nblk = bins // LANES
+    each = C * nblk
+    hrows = own * each
+    total = chunks[0]
     lanes = lax.broadcasted_iota(jnp.int32, total[hrows:].shape, 1)
     hsum, ssum = total[:hrows], total[hrows:]
-    for d in range(1, n):
-        got = rotate(lax.dynamic_index_in_dim(chunks, (me + d) % n, 0, False), "ep", d)
-        hsum = hsum + got[:hrows]
-        ssum = jnp.where(lanes >= 16 * series, jnp.minimum(ssum, got[hrows:]), ssum + got[hrows:])
+    for d in range(1, rest):
+        piece = rotate(chunks[d], "ep", 2 * d)
+        hsum = hsum + piece[:hrows]
+        ssum = jnp.where(lanes >= 32 * half, jnp.minimum(ssum, piece[hrows:]), ssum + piece[hrows:])
     mine = jnp.concatenate([hsum * density, ssum], axis=0)
-    full = jnp.zeros((n, hrows, LANES), jnp.float32)
-    sfull = jnp.zeros((n,) + ssum.shape, jnp.float32)
-    for d in range(n):
-        got = rotate(mine, "ep", d) if d else mine
-        full = lax.dynamic_update_index_in_dim(full, got[:hrows], (me - d) % n, 0)
-        sfull = lax.dynamic_update_index_in_dim(sfull, got[hrows:], (me - d) % n, 0)
-    part_hist = (
-        full.reshape(GROUPS, C, bins // LANES, 2, LANES).transpose(0, 1, 3, 2, 4).reshape(GROUPS, C, 2, bins)
-    )
-    stats = sfull[:, :own].reshape(GROUPS, LANES)
-    part_tns, part_share, tns, wns = run_small(stats, C, endpoints)
+    pieces = [rotate(mine, "ep", d) if d else mine for d in range(n)]
+    full, part_tns, part_share, tns, wns = run_final(me.reshape(1), pieces, C, own, 2 * each, endpoints)
+    part_hist = full.reshape(GROUPS, C, nblk, 2, LANES).transpose(0, 1, 3, 2, 4).reshape(GROUPS, C, 2, bins)
     part_tns = part_tns.transpose(2, 0, 1)
     part_share = part_share.reshape(GROUPS)
     return (part_hist, part_tns, part_share, tns, wns, worst)

time: 69.3 us -> 57.3 us (0.83)
  waiting for transfers between devices: 31.1 us -> 10.1 us
  starting transfers between devices: 14.5 us -> 20.8 us
  Pallas kernels: 18.1 us -> 21.1 us
    ppermute x17 -> x13, waiting for transfers between devices: 31.1 us -> 7.81 us  [rotate(): lax.ppermute(value, axis, [(i, (i + distance) % size) for i in range(size)])]
    ppermute x17 -> x13, starting transfers between devices: 14.5 us -> 19.3 us  [rotate(): lax.ppermute(value, axis, [(i, (i + distance) % size) for i in range(size)])]
    pallas_call x3 -> x4, Pallas kernels: 18.1 us -> 21.1 us  [the longest x2 15.8 us: run_hist(): pl.pallas_call(functools.partial(hist_kernel, C, KT, n), in_specs=[smem,...]
    ppermute x0 -> x1, waiting for transfers between devices: none -> 2.27 us  [on_device(): got = lax.ppermute(send, 'ep', [(i, i ^ 1) for i in range(n)])]
    dynamic_update_slice x2 -> x0, other arithmetic: 1.63 us -> none  [the longest x1 0.93 us: on_device(): full = lax.dynamic_update_index_in_dim(full, got[:hrows], (me - d) % n, 0)]
    ppermute x0 -> x1, starting transfers between devices: none -> 1.49 us  [on_device(): got = lax.ppermute(send, 'ep', [(i, i ^ 1) for i in range(n)])]
    squeeze x1 -> x0, local copies, waits for them, and re-layouts: 1.12 us -> none  [on_device(): lax.dynamic_index_in_dim(chunks, (me + d) % n, 0, False)]
    mul x0 -> x1, other arithmetic: none -> 0.86 us  [on_device(): mine = jnp.concatenate([hsum * density, ssum], axis=0)]
  transfers between devices with their start and end apart: 17 -> 14, of which waited for: 7 -> 6; matrix products, arithmetic and copies ran while one was open for 0% -> 4% of each run, Pallas kernels for 2% -> 28%
where the time goes in v2:
time: 57.3 us; the launch traced here: 56.4 us
  Pallas kernels  21.1 us (37%)
  starting transfers between devices  20.8 us (36%)
  waiting for transfers between devices  10.1 us (18%)
  other arithmetic  2.36 us (4%)
  local copies, waits for them, and re-layouts  1.38 us (2%)
  between operations  0.71 us (1%)
    ppermute x13, starting transfers between devices, rotate(): lax.ppermute(value, axis, [(i, (i + distance) % size) for i in range(size)])  19.3 us
    pallas_call x2, Pallas kernels, run_hist(): pl.pallas_call(functools.partial(hist_kernel, C, KT, n), in_specs=[smem,...  15.8 us
    ppermute x13, waiting for transfers between devices, rotate(): lax.ppermute(value, axis, [(i, (i + distance) % size) for i in range(size)])  7.81 us
    pallas_call x1, Pallas kernels, run_prep(): pl.pallas_call(functools.partial(prep_kernel, C), in_specs=[smem, smem] +...  3.38 us
    ppermute x1, waiting for transfers between devices, on_device(): got = lax.ppermute(send, 'ep', [(i, i ^ 1) for i in range(n)])  2.27 us
    pallas_call x1, Pallas kernels, run_final(): pl.pallas_call(functools.partial(final_kernel, C, own, GROUPS / endpoints...  1.99 us
    ppermute x1, starting transfers between devices, on_device(): got = lax.ppermute(send, 'ep', [(i, i ^ 1) for i in range(n)])  1.49 us
    unnamed x20, local copies, waits for them, and re-layouts  1.38 us
  transfers between devices with their start and end apart: 14, of which 6 were waited for; matrix products, arithmetic and copies ran while one was open for 4% of the time, Pallas kernels for 28%

profile of v2, /device:TPU:0, one launch (start us, length us, event | category | flops | bytes accessed | tf_op | source)
XLA Modules:
  0.0 56.4 jit_solution(11758864002818918363)
XLA Ops:
  0.6 3.4 %prep.1 = (s32[4,128]{1,0:T(4,128)}, s32[4,128]{1,0:T(4,128)}, f32[512,128]{1,0:T(8,128)}, f32[3,256,128]{2,1,0:T(8,128)}, f32[3,256,128]{2,1,0:T(8,128)}) custom-call(s32[512]{0:T(512)} %edges_ref.5, s32[1]{0:T(128)} %bitcast.2.side_ref, s32[4,128]{1,0:T(4,128)} %bitcast.43, s32[256,128]{1,0:T(8,128)} %bitcast.42, f32[512,128]{1,0:T(8,128)} %bitcast.38, ...), custom_call_target="tpu_custom_call" | custom-call | tf_op jit(solution)/shard_map/prep/pallas_call | solution.py:113
  4.0 2.4 %collective-permute-start.13 = (f32[512,128]{1,0:T(8,128)}, f32[512,128]{1,0:T(8,128)S(1)}, u32[]{:S(2)}, u32[]{:S(2)}) collective-permute-start(f32[512,128]{1,0:T(8,128)} %get-tuple-element.37), channel_id=1, source_target_pairs={{0,3},{1,0},{2,1},{3,2},{4,7},{5,4},{6,5},{7,6},{8,11},{9,8},{10,9... | collective-permute-start | bytes 786440 | tf_op jit(solution)/shard_map/ppermute | solution.py:332
  6.5 0.6 %collective-permute-start.12 = (f32[512,128]{1,0:T(8,128)}, f32[512,128]{1,0:T(8,128)S(1)}, u32[]{:S(2)}, u32[]{:S(2)}) collective-permute-start(f32[512,128]{1,0:T(8,128)} %get-tuple-element.37), channel_id=1, source_target_pairs={{0,2},{1,3},{2,0},{3,1},{4,6},{5,7},{6,4},{7,5},{8,10},{9,11},{10,... | collective-permute-start | bytes 786440 | tf_op jit(solution)/shard_map/ppermute | solution.py:332
  7.1 1.5 %collective-permute-start = (f32[3,256,128]{2,1,0:T(8,128)}, f32[3,256,128]{2,1,0:T(8,128)S(1)}, u32[]{:S(2)}, u32[]{:S(2)}) collective-permute-start(f32[3,256,128]{2,1,0:T(8,128)} %get-tuple-element.24), channel_id=1, source_target_pairs={{0,4},{4,0},{8,12},{12,8},{16,20},{20,16},{24,28},{28,24},{1,5},{5... | collective-permute-start | bytes 1179656 | tf_op jit(solution)/shard_map/ppermute | solution.py:355
  8.6 7.6 %hist.2 = (f32[2,144,256]{2,1,0:T(8,128)}, f32[2,8,128]{2,1,0:T(8,128)}) custom-call(s32[512]{0:T(512)} %edges_ref.5, s32[1]{0:T(128)} %bitcast.1.place_ref, s32[4,128]{1,0:T(4,128)} %get-tuple-element.22.coarse_ref, s32[4,128]{1,0:T(4,128)} %get-tuple-element.23.fine_ref, f32[3,256,128]{2,1,0:T(8,128)} %get-tuple-element.25.slack_ref), custom_call_target="tpu_custom_call" | custom-call | flops 4831838208 | bytes 786432 | tf_op jit(solution)/shard_map/hist/pallas_call | solution.py:269
  16.2 2.3 %collective-permute-done.slack_ref = f32[3,256,128]{2,1,0:T(8,128)S(1)} collective-permute-done((f32[3,256,128]{2,1,0:T(8,128)}, f32[3,256,128]{2,1,0:T(8,128)S(1)}, u32[]{:S(2)}, u32[]{:S(2)}) %collective-permute-start) | collective-permute-done | bytes 393248 | tf_op jit(solution)/shard_map/ppermute | solution.py:355
  18.5 0.0 copy-start.9
  18.5 0.7 %copy-done.9 = f32[3,256,128]{2,1,0:T(8,128)} copy-done((f32[3,256,128]{2,1,0:T(8,128)}, f32[3,256,128]{2,1,0:T(8,128)S(1)}, u32[]{:S(2)}) %copy-start.9) | copy-done | bytes 393240
  19.2 0.0 copy-start.1
  19.2 8.1 %hist.3 = (f32[144,128]{1,0:T(8,128)}, f32[144,128]{1,0:T(8,128)}, f32[144,128]{1,0:T(8,128)}, f32[144,128]{1,0:T(8,128)}, f32[2,8,128]{2,1,0:T(8,128)}) custom-call(s32[512]{0:T(512)} %edges_ref.5, s32[1]{0:T(128)} %bitcast.1.place_ref, s32[4,128]{1,0:T(4,128)} %get-tuple-element.22.coarse_ref, s32[4,128]{1,0:T(4,128)} %get-tuple-element.23.fine_ref, ...), custom_call_target="tpu_custom_call" | custom-call | flops 4831838208 | bytes 786432 | tf_op jit(solution)/shard_map/hist/pallas_call | solution.py:269
  27.3 3.6 %collective-permute-start.3 = (f32[144,128]{1,0:T(8,128)}, f32[144,128]{1,0:T(8,128)S(1)}, u32[]{:S(2)}, u32[]{:S(2)}) collective-permute-start(f32[144,128]{1,0:T(8,128)} %get-tuple-element.31), channel_id=1, source_target_pairs={{0,24},{4,28},{8,0},{12,4},{16,8},{20,12},{24,16},{28,20},{1,25},{... | collective-permute-start | bytes 221192 | tf_op jit(solution)/shard_map/ppermute | solution.py:332
  31.0 0.0 collective-permute-start.2
  31.0 1.0 %collective-permute-start.1 = (f32[144,128]{1,0:T(8,128)}, f32[144,128]{1,0:T(8,128)S(1)}, u32[]{:S(2)}, u32[]{:S(2)}) collective-permute-start(f32[144,128]{1,0:T(8,128)} %get-tuple-element.29), channel_id=1, source_target_pairs={{0,8},{4,12},{8,16},{12,20},{16,24},{20,28},{24,0},{28,4},{1,9},{5... | collective-permute-start | bytes 221192 | tf_op jit(solution)/shard_map/ppermute | solution.py:332
  32.0 1.9 %collective-permute-done.3 = f32[144,128]{1,0:T(8,128)S(1)} collective-permute-done((f32[144,128]{1,0:T(8,128)}, f32[144,128]{1,0:T(8,128)S(1)}, u32[]{:S(2)}, u32[]{:S(2)}) %collective-permute-start.3) | collective-permute-done | bytes 73760 | tf_op jit(solution)/shard_map/ppermute | solution.py:332
  33.9 0.0 copy-done.1
  33.9 0.0 collective-permute-start.11
  33.9 3.8 %collective-permute-done.2 = f32[144,128]{1,0:T(8,128)S(1)} collective-permute-done((f32[144,128]{1,0:T(8,128)}, f32[144,128]{1,0:T(8,128)S(1)}, u32[]{:S(2)}, u32[]{:S(2)}) %collective-permute-start.2) | collective-permute-done | bytes 73760 | tf_op jit(solution)/shard_map/ppermute | solution.py:332
  37.7 0.0 collective-permute-done.1
  37.7 0.9 %fusion = f32[128,128]{1,0:T(8,128)S(1)} fusion(f32[144,128]{1,0:T(8,128)S(1)} %collective-permute-done.3, f32[144,128]{1,0:T(8,128)S(1)} %collective-permute-done.2, f32[144,128]{1,0:T(8,128)S(1)} %collective-permute-done.1, f32[144,128]{1,0:T(8,128)} %get-tuple-element.28), kind=kLoop, calls=%fused_computation.3 | loop fusion | flops 65536 | bytes 327680 | tf_op jit(solution)/shard_map/mul | solution.py:373
  38.5 0.7 %add_select_fusion = f32[16,128]{1,0:T(8,128)S(1)} fusion(f32[144,128]{1,0:T(8,128)S(1)} %collective-permute-done.3, f32[144,128]{1,0:T(8,128)S(1)} %collective-permute-done.2, f32[144,128]{1,0:T(8,128)S(1)} %collective-permute-done.1, f32[144,128]{1,0:T(8,128)} %get-tuple-element.28, pred[128]{0:T(512)(128)(4,1)S(1)} %iota_compare_fusion), kind=kLoop, calls=%fused_computation.6 | loop fusion | flops 18432 | bytes 41088 | tf_op jit(solution)/shard_map/jit(_where)/select_n | solution.py:372
  39.2 0.0 copy-start
  39.3 1.5 %collective-permute-start.4 = (f32[144,128]{1,0:T(8,128)S(1)}, f32[144,128]{1,0:T(8,128)S(1)}, u32[]{:S(2)}, u32[]{:S(2)}) collective-permute-start(f32[144,128]{1,0:T(8,128)S(1)} %pad_maximum_fusion.refs_0_), channel_id=1, source_target_pairs={{0,4},{4,8},{8,12},{12,16},{16,20},{20,24},{24,28},{28,0},{1,5},{5... | collective-permute-start | bytes 221192 | tf_op jit(solution)/shard_map/ppermute | solution.py:332
  40.8 0.1 collective-permute-start.5
  40.9 0.0 collective-permute-done.13
  40.9 2.4 %collective-permute-start.6 = (f32[144,128]{1,0:T(8,128)S(1)}, f32[144,128]{1,0:T(8,128)S(1)}, u32[]{:S(2)}, u32[]{:S(2)}) collective-permute-start(f32[144,128]{1,0:T(8,128)S(1)} %pad_maximum_fusion.refs_0_), channel_id=1, source_target_pairs={{0,12},{4,16},{8,20},{12,24},{16,28},{20,0},{24,4},{28,8},{1,13},{... | collective-permute-start | bytes 221192 | tf_op jit(solution)/shard_map/ppermute | solution.py:332
  43.3 0.0 collective-permute-done.12
  43.3 1.4 %collective-permute-start.7 = (f32[144,128]{1,0:T(8,128)S(1)}, f32[144,128]{1,0:T(8,128)S(1)}, u32[]{:S(2)}, u32[]{:S(2)}) collective-permute-start(f32[144,128]{1,0:T(8,128)S(1)} %pad_maximum_fusion.refs_0_), channel_id=1, source_target_pairs={{0,16},{4,20},{8,24},{12,28},{16,0},{20,4},{24,8},{28,12},{1,17},{... | collective-permute-start | bytes 221192 | tf_op jit(solution)/shard_map/ppermute | solution.py:332
  44.7 0.0 collective-permute-done.11
  44.7 2.4 %collective-permute-start.8 = (f32[144,128]{1,0:T(8,128)S(1)}, f32[144,128]{1,0:T(8,128)S(1)}, u32[]{:S(2)}, u32[]{:S(2)}) collective-permute-start(f32[144,128]{1,0:T(8,128)S(1)} %pad_maximum_fusion.refs_0_), channel_id=1, source_target_pairs={{0,20},{4,24},{8,28},{12,0},{16,4},{20,8},{24,12},{28,16},{1,21},{... | collective-permute-start | bytes 221192 | tf_op jit(solution)/shard_map/ppermute | solution.py:332
  47.2 0.0 collective-permute-done.4.refs_1_
  47.2 0.0 copy-start.2
  47.2 2.3 %collective-permute-start.9 = (f32[144,128]{1,0:T(8,128)S(1)}, f32[144,128]{1,0:T(8,128)S(1)}, u32[]{:S(2)}, u32[]{:S(2)}) collective-permute-start(f32[144,128]{1,0:T(8,128)S(1)} %pad_maximum_fusion.refs_0_), channel_id=1, source_target_pairs={{0,24},{4,28},{8,0},{12,4},{16,8},{20,12},{24,16},{28,20},{1,25},{... | collective-permute-start | bytes 221192 | tf_op jit(solution)/shard_map/ppermute | solution.py:332
  49.5 0.0 collective-permute-done.5.refs_2_
  49.5 0.0 copy-start.3
  49.5 1.4 %collective-permute-start.10 = (f32[144,128]{1,0:T(8,128)S(1)}, f32[144,128]{1,0:T(8,128)S(1)}, u32[]{:S(2)}, u32[]{:S(2)}) collective-permute-start(f32[144,128]{1,0:T(8,128)S(1)} %pad_maximum_fusion.refs_0_), channel_id=1, source_target_pairs={{0,28},{4,0},{8,4},{12,8},{16,12},{20,16},{24,20},{28,24},{1,29},{... | collective-permute-start | bytes 221192 | tf_op jit(solution)/shard_map/ppermute | solution.py:332
  50.9 0.8 %minimum_minimum_fusion = f32[512,128]{1,0:T(8,128)} fusion(f32[512,128]{1,0:T(8,128)S(1)} %collective-permute-done.13, f32[512,128]{1,0:T(8,128)S(1)} %collective-permute-done.12, f32[512,128]{1,0:T(8,128)S(1)} %copy-done.1, f32[512,128]{1,0:T(8,128)S(1)} %collective-permute-done.11), kind=kLoop, calls=%fused_computation | loop fusion | flops 196608 | bytes 1310720 | tf_op jit(solution)/shard_map/min | solution.py:359
  51.7 0.0 copy-done
  51.7 0.0 copy-done.2
  51.7 0.0 copy-done.3
  51.7 0.2 collective-permute-done.6.refs_3_
  51.9 0.0 copy-start.4
  51.9 1.2 %collective-permute-done.7.refs_4_ = f32[144,128]{1,0:T(8,128)S(1)} collective-permute-done((f32[144,128]{1,0:T(8,128)S(1)}, f32[144,128]{1,0:T(8,128)S(1)}, u32[]{:S(2)}, u32[]{:S(2)}) %collective-permute-start.7) | collective-permute-done | bytes 73760 | tf_op jit(solution)/shard_map/ppermute | solution.py:332
  53.0 0.0 copy-start.5
  53.1 0.0 collective-permute-done.8.refs_5_
  53.1 0.0 copy-start.6
  53.1 0.0 collective-permute-done.9.refs_6_
  53.1 0.0 copy-start.7
  53.1 0.7 %collective-permute-done.10.refs_7_ = f32[144,128]{1,0:T(8,128)S(1)} collective-permute-done((f32[144,128]{1,0:T(8,128)S(1)}, f32[144,128]{1,0:T(8,128)S(1)}, u32[]{:S(2)}, u32[]{:S(2)}) %collective-permute-start.10) | collective-permute-done | bytes 73760 | tf_op jit(solution)/shard_map/ppermute | solution.py:332
  53.8 0.0 copy-start.8
  53.8 0.0 copy-done.4
  53.8 0.0 copy-done.5
  53.8 0.0 copy-done.6
  53.8 0.0 copy-done.7
  53.8 0.6 %copy-done.8 = f32[144,128]{1,0:T(8,128)} copy-done((f32[144,128]{1,0:T(8,128)}, f32[144,128]{1,0:T(8,128)S(1)}, u32[]{:S(2)}) %copy-start.8) | copy-done | bytes 73752
  54.4 2.0 %final.1 = (f32[1024,128]{1,0:T(8,128)}, f32[2,2,64]{2,1,0:T(2,128)}, f32[1,64]{1,0:T(1,128)}, f32[2,2]{1,0:T(2,128)}, f32[2,2]{1,0:T(2,128)}) custom-call(s32[1]{0:T(128)} %bitcast.me_ref, f32[144,128]{1,0:T(8,128)} %copy-done, f32[144,128]{1,0:T(8,128)} %copy-done.2, f32[144,128]{1,0:T(8,128)} %copy-done.3, f32[144,128]{1,0:T(8,128)} %copy-done.4, ...), custom_call_target="tpu_custom_call" | custom-call | tf_op jit(solution)/shard_map/final/pallas_call | solution.py:315
  (2 shorter events, 0.0 us)
Async XLA Ops:
  4.0 36.9 %collective-permute-start.13 = (f32[512,128]{1,0:T(8,128)}, f32[512,128]{1,0:T(8,128)S(1)}, u32[]{:S(2)}, u32[]{:S(2)}) collective-permute-start(f32[512,128]{1,0:T(8,128)} %get-tuple-element.37), channel_id=1, source_target_pairs={{0,3},{1,0},{2,1},{3,2},{4,7},{5,4},{6,5},{7,6},{8,11},{9,8},{10,9... | collective-permute-start | bytes 786440 | tf_op jit(solution)/shard_map/ppermute | solution.py:332
  6.5 36.9 %collective-permute-start.12 = (f32[512,128]{1,0:T(8,128)}, f32[512,128]{1,0:T(8,128)S(1)}, u32[]{:S(2)}, u32[]{:S(2)}) collective-permute-start(f32[512,128]{1,0:T(8,128)} %get-tuple-element.37), channel_id=1, source_target_pairs={{0,2},{1,3},{2,0},{3,1},{4,6},{5,7},{6,4},{7,5},{8,10},{9,11},{10,... | collective-permute-start | bytes 786440 | tf_op jit(solution)/shard_map/ppermute | solution.py:332
  7.1 11.4 %collective-permute-start = (f32[3,256,128]{2,1,0:T(8,128)}, f32[3,256,128]{2,1,0:T(8,128)S(1)}, u32[]{:S(2)}, u32[]{:S(2)}) collective-permute-start(f32[3,256,128]{2,1,0:T(8,128)} %get-tuple-element.24), channel_id=1, source_target_pairs={{0,4},{4,0},{8,12},{12,8},{16,20},{20,16},{24,28},{28,24},{1,5},{5... | collective-permute-start | bytes 1179656 | tf_op jit(solution)/shard_map/ppermute | solution.py:355
  18.5 0.7 %copy-start.9 = (f32[3,256,128]{2,1,0:T(8,128)}, f32[3,256,128]{2,1,0:T(8,128)S(1)}, u32[]{:S(2)}) copy-start(f32[3,256,128]{2,1,0:T(8,128)S(1)} %collective-permute-done.slack_ref) | copy-start | bytes 1179652
  19.2 14.6 %copy-start.1 = (f32[512,128]{1,0:T(8,128)S(1)}, f32[512,128]{1,0:T(8,128)}, u32[]{:S(2)}) copy-start(f32[512,128]{1,0:T(8,128)} %get-tuple-element.37) | copy-start | bytes 786436
  27.3 6.5 %collective-permute-start.3 = (f32[144,128]{1,0:T(8,128)}, f32[144,128]{1,0:T(8,128)S(1)}, u32[]{:S(2)}, u32[]{:S(2)}) collective-permute-start(f32[144,128]{1,0:T(8,128)} %get-tuple-element.31), channel_id=1, source_target_pairs={{0,24},{4,28},{8,0},{12,4},{16,8},{20,12},{24,16},{28,20},{1,25},{... | collective-permute-start | bytes 221192 | tf_op jit(solution)/shard_map/ppermute | solution.py:332
  31.0 6.7 %collective-permute-start.2 = (f32[144,128]{1,0:T(8,128)}, f32[144,128]{1,0:T(8,128)S(1)}, u32[]{:S(2)}, u32[]{:S(2)}) collective-permute-start(f32[144,128]{1,0:T(8,128)} %get-tuple-element.30), channel_id=1, source_target_pairs={{0,16},{4,20},{8,24},{12,28},{16,0},{20,4},{24,8},{28,12},{1,17},{... | collective-permute-start | bytes 221192 | tf_op jit(solution)/shard_map/ppermute | solution.py:332
  31.0 6.7 %collective-permute-start.1 = (f32[144,128]{1,0:T(8,128)}, f32[144,128]{1,0:T(8,128)S(1)}, u32[]{:S(2)}, u32[]{:S(2)}) collective-permute-start(f32[144,128]{1,0:T(8,128)} %get-tuple-element.29), channel_id=1, source_target_pairs={{0,8},{4,12},{8,16},{12,20},{16,24},{20,28},{24,0},{28,4},{1,9},{5... | collective-permute-start | bytes 221192 | tf_op jit(solution)/shard_map/ppermute | solution.py:332
  33.9 10.9 %collective-permute-start.11 = (f32[512,128]{1,0:T(8,128)S(1)}, f32[512,128]{1,0:T(8,128)S(1)}, u32[]{:S(2)}, u32[]{:S(2)}) collective-permute-start(f32[512,128]{1,0:T(8,128)S(1)} %copy-done.1), channel_id=1, source_target_pairs={{0,1},{1,2},{2,3},{3,0},{4,5},{5,6},{6,7},{7,4},{8,9},{9,10},{10,1... | collective-permute-start | bytes 786440 | tf_op jit(solution)/shard_map/ppermute | solution.py:332
  39.2 12.4 %copy-start = (f32[144,128]{1,0:T(8,128)}, f32[144,128]{1,0:T(8,128)S(1)}, u32[]{:S(2)}) copy-start(f32[144,128]{1,0:T(8,128)S(1)} %pad_maximum_fusion.refs_0_) | copy-start | bytes 221188
  39.3 7.9 %collective-permute-start.4 = (f32[144,128]{1,0:T(8,128)S(1)}, f32[144,128]{1,0:T(8,128)S(1)}, u32[]{:S(2)}, u32[]{:S(2)}) collective-permute-start(f32[144,128]{1,0:T(8,128)S(1)} %pad_maximum_fusion.refs_0_), channel_id=1, source_target_pairs={{0,4},{4,8},{8,12},{12,16},{16,20},{20,24},{24,28},{28,0},{1,5},{5... | collective-permute-start | bytes 221192 | tf_op jit(solution)/shard_map/ppermute | solution.py:332
  40.8 8.7 %collective-permute-start.5 = (f32[144,128]{1,0:T(8,128)S(1)}, f32[144,128]{1,0:T(8,128)S(1)}, u32[]{:S(2)}, u32[]{:S(2)}) collective-permute-start(f32[144,128]{1,0:T(8,128)S(1)} %pad_maximum_fusion.refs_0_), channel_id=1, source_target_pairs={{0,8},{4,12},{8,16},{12,20},{16,24},{20,28},{24,0},{28,4},{1,9},{5... | collective-permute-start | bytes 221192 | tf_op jit(solution)/shard_map/ppermute | solution.py:332
  40.9 10.9 %collective-permute-start.6 = (f32[144,128]{1,0:T(8,128)S(1)}, f32[144,128]{1,0:T(8,128)S(1)}, u32[]{:S(2)}, u32[]{:S(2)}) collective-permute-start(f32[144,128]{1,0:T(8,128)S(1)} %pad_maximum_fusion.refs_0_), channel_id=1, source_target_pairs={{0,12},{4,16},{8,20},{12,24},{16,28},{20,0},{24,4},{28,8},{1,13},{... | collective-permute-start | bytes 221192 | tf_op jit(solution)/shard_map/ppermute | solution.py:332
  43.3 9.7 %collective-permute-start.7 = (f32[144,128]{1,0:T(8,128)S(1)}, f32[144,128]{1,0:T(8,128)S(1)}, u32[]{:S(2)}, u32[]{:S(2)}) collective-permute-start(f32[144,128]{1,0:T(8,128)S(1)} %pad_maximum_fusion.refs_0_), channel_id=1, source_target_pairs={{0,16},{4,20},{8,24},{12,28},{16,0},{20,4},{24,8},{28,12},{1,17},{... | collective-permute-start | bytes 221192 | tf_op jit(solution)/shard_map/ppermute | solution.py:332
  44.7 8.3 %collective-permute-start.8 = (f32[144,128]{1,0:T(8,128)S(1)}, f32[144,128]{1,0:T(8,128)S(1)}, u32[]{:S(2)}, u32[]{:S(2)}) collective-permute-start(f32[144,128]{1,0:T(8,128)S(1)} %pad_maximum_fusion.refs_0_), channel_id=1, source_target_pairs={{0,20},{4,24},{8,28},{12,0},{16,4},{20,8},{24,12},{28,16},{1,21},{... | collective-permute-start | bytes 221192 | tf_op jit(solution)/shard_map/ppermute | solution.py:332
  47.2 4.5 %copy-start.2 = (f32[144,128]{1,0:T(8,128)}, f32[144,128]{1,0:T(8,128)S(1)}, u32[]{:S(2)}) copy-start(f32[144,128]{1,0:T(8,128)S(1)} %collective-permute-done.4.refs_1_) | copy-start | bytes 221188
  47.2 5.9 %collective-permute-start.9 = (f32[144,128]{1,0:T(8,128)S(1)}, f32[144,128]{1,0:T(8,128)S(1)}, u32[]{:S(2)}, u32[]{:S(2)}) collective-permute-start(f32[144,128]{1,0:T(8,128)S(1)} %pad_maximum_fusion.refs_0_), channel_id=1, source_target_pairs={{0,24},{4,28},{8,0},{12,4},{16,8},{20,12},{24,16},{28,20},{1,25},{... | collective-permute-start | bytes 221192 | tf_op jit(solution)/shard_map/ppermute | solution.py:332
  49.5 2.2 %copy-start.3 = (f32[144,128]{1,0:T(8,128)}, f32[144,128]{1,0:T(8,128)S(1)}, u32[]{:S(2)}) copy-start(f32[144,128]{1,0:T(8,128)S(1)} %collective-permute-done.5.refs_2_) | copy-start | bytes 221188
  49.5 4.4 %collective-permute-start.10 = (f32[144,128]{1,0:T(8,128)S(1)}, f32[144,128]{1,0:T(8,128)S(1)}, u32[]{:S(2)}, u32[]{:S(2)}) collective-permute-start(f32[144,128]{1,0:T(8,128)S(1)} %pad_maximum_fusion.refs_0_), channel_id=1, source_target_pairs={{0,28},{4,0},{8,4},{12,8},{16,12},{20,16},{24,20},{28,24},{1,29},{... | collective-permute-start | bytes 221192 | tf_op jit(solution)/shard_map/ppermute | solution.py:332
  51.9 1.9 %copy-start.4 = (f32[144,128]{1,0:T(8,128)}, f32[144,128]{1,0:T(8,128)S(1)}, u32[]{:S(2)}) copy-start(f32[144,128]{1,0:T(8,128)S(1)} %collective-permute-done.6.refs_3_) | copy-start | bytes 221188
  53.0 0.8 %copy-start.5 = (f32[144,128]{1,0:T(8,128)}, f32[144,128]{1,0:T(8,128)S(1)}, u32[]{:S(2)}) copy-start(f32[144,128]{1,0:T(8,128)S(1)} %collective-permute-done.7.refs_4_) | copy-start | bytes 221188
  53.1 0.8 %copy-start.6 = (f32[144,128]{1,0:T(8,128)}, f32[144,128]{1,0:T(8,128)S(1)}, u32[]{:S(2)}) copy-start(f32[144,128]{1,0:T(8,128)S(1)} %collective-permute-done.8.refs_5_) | copy-start | bytes 221188
  53.1 0.8 %copy-start.7 = (f32[144,128]{1,0:T(8,128)}, f32[144,128]{1,0:T(8,128)S(1)}, u32[]{:S(2)}) copy-start(f32[144,128]{1,0:T(8,128)S(1)} %collective-permute-done.9.refs_6_) | copy-start | bytes 221188
  53.8 0.6 %copy-start.8 = (f32[144,128]{1,0:T(8,128)}, f32[144,128]{1,0:T(8,128)S(1)}, u32[]{:S(2)}) copy-start(f32[144,128]{1,0:T(8,128)S(1)} %collective-permute-done.10.refs_7_) | copy-start | bytes 221188

commit v3 on v2

--- a/solution.py
+++ b/solution.py
@@ -12,6 +12,8 @@
 F8 = jnp.float8_e4m3fn
 BF = jnp.bfloat16
 STEP = 0.001
+VMEM = 12 << 20
+EXTRA = 8
 
 
 def lookup(table_ref, index):
@@ -56,9 +58,14 @@
 
 
 def prep_kernel(
-    C, edges_ref, side_ref, lines_ref, ids_ref, a_ref, b_ref, c_ref, d_ref,
-    coarse_ref, fine_ref, worst_ref, keep_ref, send_ref,
+    C, edges_ref, side_ref, lines_ref, *refs
 ):
+    sources, refs = refs[:5], refs[5:]
+    (coarse_ref, fine_ref, worst_ref, keep_ref, send_ref), held, sems = refs[:5], refs[5:10], refs[10]
+    copies = [pltpu.make_async_copy(src, dst, sems.at[i]) for i, (src, dst) in enumerate(zip(sources, held))]
+    for copy in copies:
+        copy.start()
+    ids_ref, a_ref, b_ref, c_ref, d_ref = held
     bins = edges_ref.shape[0]
     cell = lax.broadcasted_iota(jnp.int32, coarse_ref.shape, 0) * LANES + lax.broadcasted_iota(
         jnp.int32, coarse_ref.shape, 1
@@ -86,6 +93,8 @@
     following = jnp.where(last, below, left)
     fine_ref[...] = q + (following - q) * 65536
 
+    for copy in copies:
+        copy.wait()
     flag = side_ref[0] == 0
     half = C // 2
     lines = a_ref.shape[0] // C
@@ -112,7 +121,7 @@
     smem = pl.BlockSpec(memory_space=pltpu.SMEM)
     return pl.pallas_call(
         functools.partial(prep_kernel, C),
-        in_specs=[smem, smem] + [pl.BlockSpec(memory_space=pltpu.VMEM)] * 6,
+        in_specs=[smem, smem, pl.BlockSpec(memory_space=pltpu.VMEM)] + [pl.BlockSpec(memory_space=pltpu.HBM)] * 5,
         out_shape=[
             jax.ShapeDtypeStruct((LEAST // 8 // LANES, LANES), jnp.int32),
             jax.ShapeDtypeStruct((bins // LANES, LANES), jnp.int32),
@@ -120,8 +129,10 @@
             jax.ShapeDtypeStruct((3, lines * C // 2, LANES), jnp.float32),
             jax.ShapeDtypeStruct((3, lines * C // 2, LANES), jnp.float32),
         ],
+        scratch_shapes=[pltpu.VMEM(x.shape, x.dtype) for x in (ids, a, b, c, d)] + [pltpu.SemaphoreType.DMA((5,))],
+        compiler_params=pltpu.CompilerParams(vmem_limit_bytes=VMEM),
         name="prep",
-    )(edges, side, edges.reshape(-1, LANES), ids, a, b, c, d)
+    )(edges, side, pltpu.with_memory_space_constraint(edges.reshape(-1, LANES), pltpu.HBM), ids, a, b, c, d)
 
 
 def hist_kernel(C, KT, n, edges_ref, place_ref, coarse_ref, fine_ref, slack_ref, *refs):
@@ -213,38 +224,43 @@
 
         lax.fori_loop(0, chunks // 2, two, 0)
 
-        stats, lane = [], lax.broadcasted_iota(jnp.int32, (GROUPS, LANES), 1)
         sums = [pltpu.matmul_pop(a) for a in accs]
         if not n:
             for s in range(series):
                 out_ref[s] = sums[s]
             return
-        sums = [prior_ref[s] + sums[s] for s in range(series)]
         own = GROUPS // n
-        for out in sums:
-            stats.append(out[LANES:])
-        stats.append(jnp.zeros((LANES - 16 * series, nblk * GROUPS), jnp.float32))
-        turned = jnp.concatenate(stats, axis=0).T
-        total = sum(turned[h * GROUPS:(h + 1) * GROUPS] for h in range(nblk))
-        sub8 = lax.broadcasted_iota(jnp.int32, (8, LANES), 0)
-        chunk_rows = all_ref.shape[0] // n
+        lane = lax.broadcasted_iota(jnp.int32, (8, LANES), 1)
+        sub = lax.broadcasted_iota(jnp.int32, (8, LANES), 0)
+        wide_lane = lax.broadcasted_iota(jnp.int32, (8, nblk * GROUPS), 1)
+        wide_sub = lax.broadcasted_iota(jnp.int32, (8, nblk * GROUPS), 0)
+        chunk_rows = outs[0].shape[0]
         hist_rows = own * series * nblk
+        tile = jnp.zeros((8, LANES), jnp.float32)
         for s in range(series):
             c, m = divmod(s, 2)
-            low = jnp.min(jnp.where(sub8 % C == c, low_ref[m], jnp.inf), keepdims=True)
-            total = jnp.where(lane == 16 * series + s, low, total)
-            full = sums[s][:LANES].T
+            total = prior_ref[s] + sums[s]
+            stats = total[LANES:LANES + 8]
+            across = jnp.broadcast_to(pltpu.roll(stats, GROUPS, 1)[2:3], wide_lane.shape)
+            top = total[:8] + jnp.where((wide_sub == 0) & (wide_lane >= GROUPS), across, 0.0)
+            full = jnp.concatenate([top, total[8:LANES]], axis=0).T
+            folded = stats[:, :LANES]
+            for v in range(1, nblk * GROUPS // LANES):
+                folded = folded + stats[:, v * LANES:(v + 1) * LANES]
+            folded = folded + pltpu.roll(folded, GROUPS, 1)
+            low = jnp.min(jnp.where(sub % C == c, low_ref[m], jnp.inf), keepdims=True)
+            row = jnp.where(lane < GROUPS, folded[0:1] + folded[1:2], low)
+            tile = jnp.where(sub == s, row, tile)
+            if s == 0:
+                tile = jnp.where(sub == series, folded[3:4], tile)
             for h in range(nblk):
-                value = full[h * GROUPS:(h + 1) * GROUPS]
-                if h:
-                    column = turned[(h - 1) * GROUPS:h * GROUPS, 16 * s + 2:16 * s + 3]
-                    value = jnp.where(lane == 0, value + column, value)
                 for i in range(n):
                     at = i * chunk_rows + (c * nblk + h) * 2 + m
-                    all_ref[pl.ds(at, own, stride=series * nblk), :] = value[i * own:(i + 1) * own]
+                    first = h * GROUPS + i * own
+                    all_ref[pl.ds(at, own, stride=series * nblk), :] = full[first:first + own]
         for i in range(n):
             at = i * chunk_rows + hist_rows
-            all_ref[at:at + own, :] = total[i * own:(i + 1) * own]
+            all_ref[at:at + EXTRA, :] = tile
         for d in range(n):
             at = pl.multiple_of(lax.rem(place_ref[0] + d, n) * chunk_rows, 8)
             outs[d][...] = all_ref[pl.ds(at, chunk_rows), :]
@@ -261,7 +277,7 @@
     low = jax.ShapeDtypeStruct((2, 8, LANES), jnp.float32)
     if n:
         own = GROUPS // n
-        rows = own * series * nblk + own + (-own % 8)
+        rows = own * series * nblk + EXTRA
         outs = [jax.ShapeDtypeStruct((rows, LANES), jnp.float32) for _ in range(n)]
         scratch += [pltpu.VMEM((2, 8, LANES), jnp.float32)] * 0 + [pltpu.VMEM((n * rows, LANES), jnp.float32)]
     else:
@@ -274,14 +290,15 @@
         cost_estimate=pl.CostEstimate(
             flops=4 * (LANES + 16) * 256 * slack.size // 3, bytes_accessed=8 * slack.size, transcendentals=slack.size
         ),
+        compiler_params=pltpu.CompilerParams(vmem_limit_bytes=VMEM),
         name="hist",
     )(edges, place, coarse, fine, slack, *prior)
 
 
 def final_kernel(C, own, share, scale, me_ref, *refs):
-    n = len(refs) - 6
+    n = len(refs) - 5
     pieces = refs[:n]
-    hist_ref, part_ref, share_ref, tns_ref, wns_ref, stats_ref = refs[n:]
+    hist_ref, part_ref, share_ref, tns_ref, wns_ref = refs[n:]
     half = C // 2
     each = hist_ref.shape[0] // GROUPS // 2
     for d in range(n):
@@ -290,22 +307,23 @@
         for p in range(own):
             at = pl.multiple_of((place * own + p) * 2 * each + side * each, 8)
             hist_ref[pl.ds(at, each), :] = pieces[d][p * each:(p + 1) * each, :]
-        stats_ref[side, pl.ds(place * own, own), :] = pieces[d][own * each:own * each + own, :]
     tns = jnp.zeros((C, 2), jnp.float32)
     wns = jnp.zeros((C, 2), jnp.float32)
     row = lax.broadcasted_iota(jnp.int32, (C, 2), 0)
     col = lax.broadcasted_iota(jnp.int32, (C, 2), 1)
+    mine, other = pieces[0][own * each:, :], pieces[1][own * each:, :]
+    even = me_ref[0] % 2 == 0
     for side in range(2):
-        turned = stats_ref[side].T
+        tile = jnp.where(even, mine, other) if side == 0 else jnp.where(even, other, mine)
         for s in range(2 * half):
             c, m = divmod(s, 2)
             c += side * half
-            sums = turned[16 * s:16 * s + 1, :] + turned[16 * s + 1:16 * s + 2, :]
+            sums = tile[s:s + 1, :GROUPS]
             part_ref[c, m:m + 1, :] = sums * share
             here = (row == c) & (col == m)
             tns = jnp.where(here, jnp.sum(sums, keepdims=True) * scale, tns)
-            wns = jnp.where(here, turned[32 * half + s:32 * half + s + 1, :1], wns)
-    share_ref[...] = turned[3:4, :] * share
+            wns = jnp.where(here, tile[s:s + 1, GROUPS:GROUPS + 1], wns)
+    share_ref[...] = mine[2 * half:2 * half + 1, :GROUPS] * share
     tns_ref[...] = tns
     wns_ref[...] = wns
 
@@ -322,7 +340,7 @@
             jax.ShapeDtypeStruct((C, 2), jnp.float32),
             jax.ShapeDtypeStruct((C, 2), jnp.float32),
         ],
-        scratch_shapes=[pltpu.VMEM((2, GROUPS, LANES), jnp.float32)],
+        compiler_params=pltpu.CompilerParams(vmem_limit_bytes=VMEM),
         name="final",
     )(me, *pieces)
 
@@ -350,8 +368,9 @@
     rest = n // 2
     data = (tiles(required), tiles(arrival), tiles(early_arrival), tiles(hold_required))
     ids = part_ids.reshape(-1, LANES)
+    data = tuple(pltpu.with_memory_space_constraint(x, pltpu.HBM) for x in data)
     lines = ids.shape[0]
-    coarse, fine, near, keep, send = run_prep(bin_edges, side.reshape(1), ids, *data, C)
+    coarse, fine, near, keep, send = run_prep(bin_edges, side.reshape(1), pltpu.with_memory_space_constraint(ids, pltpu.HBM), *data, C)
     got = lax.ppermute(send, "ep", [(i, i ^ 1) for i in range(n)])
     shares = [rotate(near, "corner", d) for d in range(1, lax.axis_size("corner"))]
     prior = run_hist(bin_edges, place.reshape(1), coarse, fine, keep, half)
@@ -364,13 +383,13 @@
     each = C * nblk
     hrows = own * each
     total = chunks[0]
-    lanes = lax.broadcasted_iota(jnp.int32, total[hrows:].shape, 1)
-    hsum, ssum = total[:hrows], total[hrows:]
+    row = lax.broadcasted_iota(jnp.int32, total.shape, 0)
+    lane = lax.broadcasted_iota(jnp.int32, total.shape, 1)
+    least = (row >= hrows) & (row < hrows + 2 * half) & (lane >= GROUPS)
     for d in range(1, rest):
         piece = rotate(chunks[d], "ep", 2 * d)
-        hsum = hsum + piece[:hrows]
-        ssum = jnp.where(lanes >= 32 * half, jnp.minimum(ssum, piece[hrows:]), ssum + piece[hrows:])
-    mine = jnp.concatenate([hsum * density, ssum], axis=0)
+        total = jnp.where(least, jnp.minimum(total, piece), total + piece)
+    mine = jnp.where(row < hrows, total * density, total)
     pieces = [rotate(mine, "ep", d) if d else mine for d in range(n)]
     full, part_tns, part_share, tns, wns = run_final(me.reshape(1), pieces, C, own, 2 * each, endpoints)
     part_hist = full.reshape(GROUPS, C, nblk, 2, LANES).transpose(0, 1, 3, 2, 4).reshape(GROUPS, C, 2, bins)

time: 57.3 us -> 49.4 us (0.86); the launches traced: 56.4 us -> 49.1 us
  Pallas kernels: 21.1 us -> 16.2 us
  other arithmetic: 2.36 us -> 0.91 us
  local copies, waits for them, and re-layouts: 1.38 us -> 0.68 us
    pallas_call x2, Pallas kernels: 15.8 us -> 13.2 us  [run_hist(): pl.pallas_call(functools.partial(hist_kernel, C, KT, n), in_specs=[smem,...]
    pallas_call x1, Pallas kernels: 3.38 us -> 2.17 us  [run_prep(): pl.pallas_call(functools.partial(prep_kernel, C), in_specs=[smem, smem, p...]
    pallas_call x1, Pallas kernels: 1.99 us -> 0.85 us  [run_final(): pl.pallas_call(functools.partial(final_kernel, C, own, GROUPS / endpoints...]
    mul x1 -> x0, other arithmetic: 0.86 us -> none  [on_device(): mine = jnp.concatenate([hsum * density, ssum], axis=0)]
    unnamed x20 -> x2, local copies, waits for them, and re-layouts: 1.38 us -> 0.68 us
    select_n x1, other arithmetic: 0.71 us -> 0.1 us  [on_device(): mine = jnp.where(row < hrows, total * density, total)]
  transfers between devices with their start and end apart: 14 -> 14, of which waited for: 6 -> 6; matrix products, arithmetic and copies ran while one was open for 4% -> 2% of each run, Pallas kernels for 28% -> 27%
where the time goes in v3:
time: 49.4 us; the launch traced here: 49.1 us
  starting transfers between devices  20.8 us (42%)
  Pallas kernels  16.2 us (33%)
  waiting for transfers between devices  9.83 us (20%)
  other arithmetic  0.91 us (2%)
  between operations  0.69 us (1%)
  local copies, waits for them, and re-layouts  0.68 us (1%)
    ppermute x13, starting transfers between devices, rotate(): lax.ppermute(value, axis, [(i, (i + distance) % size) for i in range(size)])  19.3 us
    pallas_call x2, Pallas kernels, run_hist(): pl.pallas_call(functools.partial(hist_kernel, C, KT, n), in_specs=[smem,...  13.2 us
    ppermute x13, waiting for transfers between devices, rotate(): lax.ppermute(value, axis, [(i, (i + distance) % size) for i in range(size)])  7.31 us
    ppermute x1, waiting for transfers between devices, on_device(): got = lax.ppermute(send, 'ep', [(i, i ^ 1) for i in range(n)])  2.52 us
    pallas_call x1, Pallas kernels, run_prep(): pl.pallas_call(functools.partial(prep_kernel, C), in_specs=[smem, smem, p...  2.17 us
    ppermute x1, starting transfers between devices, on_device(): got = lax.ppermute(send, 'ep', [(i, i ^ 1) for i in range(n)])  1.49 us
  transfers between devices with their start and end apart: 14, of which 6 were waited for; matrix products, arithmetic and copies ran while one was open for 2% of the time, Pallas kernels for 27%

profile of v3, /device:TPU:0, one launch (start us, length us, event | category | flops | bytes accessed | tf_op | source)
XLA Modules:
  0.0 49.1 jit_solution(6559590962956149655)
XLA Ops:
  0.6 2.2 %prep.1 = (s32[4,128]{1,0:T(4,128)S(1)}, s32[4,128]{1,0:T(4,128)S(1)}, f32[512,128]{1,0:T(8,128)S(1)}, f32[3,256,128]{2,1,0:T(8,128)S(1)}, f32[3,256,128]{2,1,0:T(8,128)S(1)}) custom-call(s32[512]{0:T(512)} %edges_ref.5, s32[1]{0:T(128)} %bitcast.2.side_ref, s32[4,128]{1,0:T(4,128)} %bitcast.37, s32[256,128]{1,0:T(8,128)} %bitcast.43, f32[512,128]{1,0:T(8,128)} %bitcast.39, ...), custom_call_target="tpu_custom_call" | custom-call | tf_op jit(solution)/shard_map/prep/pallas_call | solution.py:122
  2.8 2.5 %collective-permute-start.13 = (f32[512,128]{1,0:T(8,128)S(1)}, f32[512,128]{1,0:T(8,128)S(1)}, u32[]{:S(2)}, u32[]{:S(2)}) collective-permute-start(f32[512,128]{1,0:T(8,128)S(1)} %get-tuple-element.37), channel_id=1, source_target_pairs={{0,3},{1,0},{2,1},{3,2},{4,7},{5,4},{6,5},{7,6},{8,11},{9,8},{10,9... | collective-permute-start | bytes 786440 | tf_op jit(solution)/shard_map/ppermute | solution.py:350
  5.3 0.6 %collective-permute-start.12 = (f32[512,128]{1,0:T(8,128)S(1)}, f32[512,128]{1,0:T(8,128)S(1)}, u32[]{:S(2)}, u32[]{:S(2)}) collective-permute-start(f32[512,128]{1,0:T(8,128)S(1)} %get-tuple-element.37), channel_id=1, source_target_pairs={{0,2},{1,3},{2,0},{3,1},{4,6},{5,7},{6,4},{7,5},{8,10},{9,11},{10,... | collective-permute-start | bytes 786440 | tf_op jit(solution)/shard_map/ppermute | solution.py:350
  5.9 1.5 %collective-permute-start = (f32[3,256,128]{2,1,0:T(8,128)S(1)}, f32[3,256,128]{2,1,0:T(8,128)S(1)}, u32[]{:S(2)}, u32[]{:S(2)}) collective-permute-start(f32[3,256,128]{2,1,0:T(8,128)S(1)} %get-tuple-element.24), channel_id=1, source_target_pairs={{0,4},{4,0},{8,12},{12,8},{16,20},{20,16},{24,28},{28,24},{1,5},{5... | collective-permute-start | bytes 1179656 | tf_op jit(solution)/shard_map/ppermute | solution.py:374
  7.4 0.0 copy-start
  7.4 0.7 %copy-done = s32[512]{0:T(512)S(1)} copy-done((s32[512]{0:T(512)S(1)}, s32[512]{0:T(512)}, u32[]{:S(2)}) %copy-start) | copy-done | bytes 2072
  8.1 6.5 %hist.2 = (f32[2,144,256]{2,1,0:T(8,128)S(1)}, f32[2,8,128]{2,1,0:T(8,128)S(1)}) custom-call(s32[512]{0:T(512)S(1)} %copy-done, s32[1]{0:T(128)} %bitcast.1.place_ref, s32[4,128]{1,0:T(4,128)S(1)} %get-tuple-element.22.coarse_ref, s32[4,128]{1,0:T(4,128)S(1)} %get-tuple-element.23.fine_ref, f32[3,256,128]{2,1,0:T(8,128)S(1)} %get-tuple-element.25.slack_ref), custom_call_target="tpu_custom_call" | custom-call | flops 4831838208 | bytes 786432 | tf_op jit(solution)/shard_map/hist/pallas_call | solution.py:285
  14.6 2.5 %collective-permute-done.slack_ref = f32[3,256,128]{2,1,0:T(8,128)S(1)} collective-permute-done((f32[3,256,128]{2,1,0:T(8,128)S(1)}, f32[3,256,128]{2,1,0:T(8,128)S(1)}, u32[]{:S(2)}, u32[]{:S(2)}) %collective-permute-start) | collective-permute-done | bytes 393248 | tf_op jit(solution)/shard_map/ppermute | solution.py:374
  17.1 6.7 %hist.3 = (f32[136,128]{1,0:T(8,128)S(1)}, f32[136,128]{1,0:T(8,128)S(1)}, f32[136,128]{1,0:T(8,128)S(1)}, f32[136,128]{1,0:T(8,128)S(1)}, f32[2,8,128]{2,1,0:T(8,128)}) custom-call(s32[512]{0:T(512)S(1)} %copy-done, s32[1]{0:T(128)} %bitcast.1.place_ref, s32[4,128]{1,0:T(4,128)S(1)} %get-tuple-element.22.coarse_ref, ...), custom_call_target="tpu_custom_call" | custom-call | flops 4831838208 | bytes 786432 | tf_op jit(solution)/shard_map/hist/pallas_call | solution.py:285
  23.8 3.7 %collective-permute-start.3 = (f32[136,128]{1,0:T(8,128)S(1)}, f32[136,128]{1,0:T(8,128)S(1)}, u32[]{:S(2)}, u32[]{:S(2)}) collective-permute-start(f32[136,128]{1,0:T(8,128)S(1)} %get-tuple-element.31), channel_id=1, source_target_pairs={{0,24},{4,28},{8,0},{12,4},{16,8},{20,12},{24,16},{28,20},{1,25},{... | collective-permute-start | bytes 208904 | tf_op jit(solution)/shard_map/ppermute | solution.py:350
  27.5 0.0 collective-permute-start.2
  27.5 1.0 %collective-permute-start.1 = (f32[136,128]{1,0:T(8,128)S(1)}, f32[136,128]{1,0:T(8,128)S(1)}, u32[]{:S(2)}, u32[]{:S(2)}) collective-permute-start(f32[136,128]{1,0:T(8,128)S(1)} %get-tuple-element.29), channel_id=1, source_target_pairs={{0,8},{4,12},{8,16},{12,20},{16,24},{20,28},{24,0},{28,4},{1,9},{5... | collective-permute-start | bytes 208904 | tf_op jit(solution)/shard_map/ppermute | solution.py:350
  28.5 1.4 %collective-permute-done.3 = f32[136,128]{1,0:T(8,128)S(1)} collective-permute-done((f32[136,128]{1,0:T(8,128)S(1)}, f32[136,128]{1,0:T(8,128)S(1)}, u32[]{:S(2)}, u32[]{:S(2)}) %collective-permute-start.3) | collective-permute-done | bytes 69664 | tf_op jit(solution)/shard_map/ppermute | solution.py:350
  29.9 0.0 collective-permute-start.11
  29.9 3.8 %collective-permute-done.2 = f32[136,128]{1,0:T(8,128)S(1)} collective-permute-done((f32[136,128]{1,0:T(8,128)S(1)}, f32[136,128]{1,0:T(8,128)S(1)}, u32[]{:S(2)}, u32[]{:S(2)}) %collective-permute-start.2) | collective-permute-done | bytes 69664 | tf_op jit(solution)/shard_map/ppermute | solution.py:350
  33.7 0.0 collective-permute-done.1
  33.7 0.1 multiply_select_fusion.refs_0_
  33.8 1.5 %collective-permute-start.4 = (f32[136,128]{1,0:T(8,128)S(1)}, f32[136,128]{1,0:T(8,128)S(1)}, u32[]{:S(2)}, u32[]{:S(2)}) collective-permute-start(f32[136,128]{1,0:T(8,128)S(1)} %multiply_select_fusion.refs_0_), channel_id=1, source_target_pairs={{0,4},{4,8},{8,12},{12,16},{16,20},{20,24},{24,28},{28,0},{1,5},{5... | collective-permute-start | bytes 208904 | tf_op jit(solution)/shard_map/ppermute | solution.py:350
  35.4 0.1 collective-permute-start.5
  35.5 0.0 collective-permute-done.13
  35.5 2.3 %collective-permute-start.6 = (f32[136,128]{1,0:T(8,128)S(1)}, f32[136,128]{1,0:T(8,128)S(1)}, u32[]{:S(2)}, u32[]{:S(2)}) collective-permute-start(f32[136,128]{1,0:T(8,128)S(1)} %multiply_select_fusion.refs_0_), channel_id=1, source_target_pairs={{0,12},{4,16},{8,20},{12,24},{16,28},{20,0},{24,4},{28,8},{1,13},{... | collective-permute-start | bytes 208904 | tf_op jit(solution)/shard_map/ppermute | solution.py:350
  37.9 0.0 collective-permute-done.12
  37.9 1.5 %collective-permute-start.7 = (f32[136,128]{1,0:T(8,128)S(1)}, f32[136,128]{1,0:T(8,128)S(1)}, u32[]{:S(2)}, u32[]{:S(2)}) collective-permute-start(f32[136,128]{1,0:T(8,128)S(1)} %multiply_select_fusion.refs_0_), channel_id=1, source_target_pairs={{0,16},{4,20},{8,24},{12,28},{16,0},{20,4},{24,8},{28,12},{1,17},{... | collective-permute-start | bytes 208904 | tf_op jit(solution)/shard_map/ppermute | solution.py:350
  39.3 0.0 collective-permute-done.11
  39.3 2.4 %collective-permute-start.8 = (f32[136,128]{1,0:T(8,128)S(1)}, f32[136,128]{1,0:T(8,128)S(1)}, u32[]{:S(2)}, u32[]{:S(2)}) collective-permute-start(f32[136,128]{1,0:T(8,128)S(1)} %multiply_select_fusion.refs_0_), channel_id=1, source_target_pairs={{0,20},{4,24},{8,28},{12,0},{16,4},{20,8},{24,12},{28,16},{1,21},{... | collective-permute-start | bytes 208904 | tf_op jit(solution)/shard_map/ppermute | solution.py:350
  41.7 0.0 collective-permute-done.4.refs_1_
  41.7 2.2 %collective-permute-start.9 = (f32[136,128]{1,0:T(8,128)S(1)}, f32[136,128]{1,0:T(8,128)S(1)}, u32[]{:S(2)}, u32[]{:S(2)}) collective-permute-start(f32[136,128]{1,0:T(8,128)S(1)} %multiply_select_fusion.refs_0_), channel_id=1, source_target_pairs={{0,24},{4,28},{8,0},{12,4},{16,8},{20,12},{24,16},{28,20},{1,25},{... | collective-permute-start | bytes 208904 | tf_op jit(solution)/shard_map/ppermute | solution.py:350
  43.9 0.0 collective-permute-done.5.refs_2_
  43.9 1.4 %collective-permute-start.10 = (f32[136,128]{1,0:T(8,128)S(1)}, f32[136,128]{1,0:T(8,128)S(1)}, u32[]{:S(2)}, u32[]{:S(2)}) collective-permute-start(f32[136,128]{1,0:T(8,128)S(1)} %multiply_select_fusion.refs_0_), channel_id=1, source_target_pairs={{0,28},{4,0},{8,4},{12,8},{16,12},{20,16},{24,20},{28,24},{1,29},{... | collective-permute-start | bytes 208904 | tf_op jit(solution)/shard_map/ppermute | solution.py:350
  45.4 0.8 %minimum_minimum_fusion = f32[512,128]{1,0:T(8,128)} fusion(f32[512,128]{1,0:T(8,128)S(1)} %collective-permute-done.13, f32[512,128]{1,0:T(8,128)S(1)} %collective-permute-done.12, f32[512,128]{1,0:T(8,128)S(1)} %get-tuple-element.37, f32[512,128]{1,0:T(8,128)S(1)} %collective-permute-done.11), kind=kLoop, calls=%fused_computation | loop fusion | flops 196608 | bytes 1310720 | tf_op jit(solution)/shard_map/min | solution.py:378
  46.2 0.1 collective-permute-done.6.refs_3_
  46.2 1.0 %collective-permute-done.7.refs_4_ = f32[136,128]{1,0:T(8,128)S(1)} collective-permute-done((f32[136,128]{1,0:T(8,128)S(1)}, f32[136,128]{1,0:T(8,128)S(1)}, u32[]{:S(2)}, u32[]{:S(2)}) %collective-permute-start.7) | collective-permute-done | bytes 69664 | tf_op jit(solution)/shard_map/ppermute | solution.py:350
  47.2 0.0 collective-permute-done.8.refs_5_
  47.2 0.0 collective-permute-done.9.refs_6_
  47.2 1.1 %collective-permute-done.10.refs_7_ = f32[136,128]{1,0:T(8,128)S(1)} collective-permute-done((f32[136,128]{1,0:T(8,128)S(1)}, f32[136,128]{1,0:T(8,128)S(1)}, u32[]{:S(2)}, u32[]{:S(2)}) %collective-permute-start.10) | collective-permute-done | bytes 69664 | tf_op jit(solution)/shard_map/ppermute | solution.py:350
  48.3 0.9 %final.1 = (f32[1024,128]{1,0:T(8,128)}, f32[2,2,64]{2,1,0:T(2,128)}, f32[1,64]{1,0:T(1,128)}, f32[2,2]{1,0:T(2,128)}, f32[2,2]{1,0:T(2,128)}) custom-call(s32[1]{0:T(128)} %bitcast.me_ref, f32[136,128]{1,0:T(8,128)S(1)} %multiply_select_fusion.refs_0_, f32[136,128]{1,0:T(8,128)S(1)} %collective-permute-done.4.refs_1_, ...), custom_call_target="tpu_custom_call" | custom-call | tf_op jit(solution)/shard_map/final/pallas_call | solution.py:333
  (2 shorter events, 0.0 us)
Async XLA Ops:
  2.8 32.7 %collective-permute-start.13 = (f32[512,128]{1,0:T(8,128)S(1)}, f32[512,128]{1,0:T(8,128)S(1)}, u32[]{:S(2)}, u32[]{:S(2)}) collective-permute-start(f32[512,128]{1,0:T(8,128)S(1)} %get-tuple-element.37), channel_id=1, source_target_pairs={{0,3},{1,0},{2,1},{3,2},{4,7},{5,4},{6,5},{7,6},{8,11},{9,8},{10,9... | collective-permute-start | bytes 786440 | tf_op jit(solution)/shard_map/ppermute | solution.py:350
  5.3 32.5 %collective-permute-start.12 = (f32[512,128]{1,0:T(8,128)S(1)}, f32[512,128]{1,0:T(8,128)S(1)}, u32[]{:S(2)}, u32[]{:S(2)}) collective-permute-start(f32[512,128]{1,0:T(8,128)S(1)} %get-tuple-element.37), channel_id=1, source_target_pairs={{0,2},{1,3},{2,0},{3,1},{4,6},{5,7},{6,4},{7,5},{8,10},{9,11},{10,... | collective-permute-start | bytes 786440 | tf_op jit(solution)/shard_map/ppermute | solution.py:350
  5.9 11.2 %collective-permute-start = (f32[3,256,128]{2,1,0:T(8,128)S(1)}, f32[3,256,128]{2,1,0:T(8,128)S(1)}, u32[]{:S(2)}, u32[]{:S(2)}) collective-permute-start(f32[3,256,128]{2,1,0:T(8,128)S(1)} %get-tuple-element.24), channel_id=1, source_target_pairs={{0,4},{4,0},{8,12},{12,8},{16,20},{20,16},{24,28},{28,24},{1,5},{5... | collective-permute-start | bytes 1179656 | tf_op jit(solution)/shard_map/ppermute | solution.py:374
  7.4 0.7 %copy-start = (s32[512]{0:T(512)S(1)}, s32[512]{0:T(512)}, u32[]{:S(2)}) copy-start(s32[512]{0:T(512)} %edges_ref.5) | copy-start | bytes 6148
  23.8 6.0 %collective-permute-start.3 = (f32[136,128]{1,0:T(8,128)S(1)}, f32[136,128]{1,0:T(8,128)S(1)}, u32[]{:S(2)}, u32[]{:S(2)}) collective-permute-start(f32[136,128]{1,0:T(8,128)S(1)} %get-tuple-element.31), channel_id=1, source_target_pairs={{0,24},{4,28},{8,0},{12,4},{16,8},{20,12},{24,16},{28,20},{1,25},{... | collective-permute-start | bytes 208904 | tf_op jit(solution)/shard_map/ppermute | solution.py:350
  27.5 6.2 %collective-permute-start.2 = (f32[136,128]{1,0:T(8,128)S(1)}, f32[136,128]{1,0:T(8,128)S(1)}, u32[]{:S(2)}, u32[]{:S(2)}) collective-permute-start(f32[136,128]{1,0:T(8,128)S(1)} %get-tuple-element.30), channel_id=1, source_target_pairs={{0,16},{4,20},{8,24},{12,28},{16,0},{20,4},{24,8},{28,12},{1,17},{... | collective-permute-start | bytes 208904 | tf_op jit(solution)/shard_map/ppermute | solution.py:350
  27.5 6.2 %collective-permute-start.1 = (f32[136,128]{1,0:T(8,128)S(1)}, f32[136,128]{1,0:T(8,128)S(1)}, u32[]{:S(2)}, u32[]{:S(2)}) collective-permute-start(f32[136,128]{1,0:T(8,128)S(1)} %get-tuple-element.29), channel_id=1, source_target_pairs={{0,8},{4,12},{8,16},{12,20},{16,24},{20,28},{24,0},{28,4},{1,9},{5... | collective-permute-start | bytes 208904 | tf_op jit(solution)/shard_map/ppermute | solution.py:350
  29.9 9.4 %collective-permute-start.11 = (f32[512,128]{1,0:T(8,128)S(1)}, f32[512,128]{1,0:T(8,128)S(1)}, u32[]{:S(2)}, u32[]{:S(2)}) collective-permute-start(f32[512,128]{1,0:T(8,128)S(1)} %get-tuple-element.37), channel_id=1, source_target_pairs={{0,1},{1,2},{2,3},{3,0},{4,5},{5,6},{6,7},{7,4},{8,9},{9,10},{10,1... | collective-permute-start | bytes 786440 | tf_op jit(solution)/shard_map/ppermute | solution.py:350
  33.8 7.9 %collective-permute-start.4 = (f32[136,128]{1,0:T(8,128)S(1)}, f32[136,128]{1,0:T(8,128)S(1)}, u32[]{:S(2)}, u32[]{:S(2)}) collective-permute-start(f32[136,128]{1,0:T(8,128)S(1)} %multiply_select_fusion.refs_0_), channel_id=1, source_target_pairs={{0,4},{4,8},{8,12},{12,16},{16,20},{20,24},{24,28},{28,0},{1,5},{5... | collective-permute-start | bytes 208904 | tf_op jit(solution)/shard_map/ppermute | solution.py:350
  35.4 8.6 %collective-permute-start.5 = (f32[136,128]{1,0:T(8,128)S(1)}, f32[136,128]{1,0:T(8,128)S(1)}, u32[]{:S(2)}, u32[]{:S(2)}) collective-permute-start(f32[136,128]{1,0:T(8,128)S(1)} %multiply_select_fusion.refs_0_), channel_id=1, source_target_pairs={{0,8},{4,12},{8,16},{12,20},{16,24},{20,28},{24,0},{28,4},{1,9},{5... | collective-permute-start | bytes 208904 | tf_op jit(solution)/shard_map/ppermute | solution.py:350
  35.5 10.7 %collective-permute-start.6 = (f32[136,128]{1,0:T(8,128)S(1)}, f32[136,128]{1,0:T(8,128)S(1)}, u32[]{:S(2)}, u32[]{:S(2)}) collective-permute-start(f32[136,128]{1,0:T(8,128)S(1)} %multiply_select_fusion.refs_0_), channel_id=1, source_target_pairs={{0,12},{4,16},{8,20},{12,24},{16,28},{20,0},{24,4},{28,8},{1,13},{... | collective-permute-start | bytes 208904 | tf_op jit(solution)/shard_map/ppermute | solution.py:350
  37.9 9.3 %collective-permute-start.7 = (f32[136,128]{1,0:T(8,128)S(1)}, f32[136,128]{1,0:T(8,128)S(1)}, u32[]{:S(2)}, u32[]{:S(2)}) collective-permute-start(f32[136,128]{1,0:T(8,128)S(1)} %multiply_select_fusion.refs_0_), channel_id=1, source_target_pairs={{0,16},{4,20},{8,24},{12,28},{16,0},{20,4},{24,8},{28,12},{1,17},{... | collective-permute-start | bytes 208904 | tf_op jit(solution)/shard_map/ppermute | solution.py:350
  39.3 7.9 %collective-permute-start.8 = (f32[136,128]{1,0:T(8,128)S(1)}, f32[136,128]{1,0:T(8,128)S(1)}, u32[]{:S(2)}, u32[]{:S(2)}) collective-permute-start(f32[136,128]{1,0:T(8,128)S(1)} %multiply_select_fusion.refs_0_), channel_id=1, source_target_pairs={{0,20},{4,24},{8,28},{12,0},{16,4},{20,8},{24,12},{28,16},{1,21},{... | collective-permute-start | bytes 208904 | tf_op jit(solution)/shard_map/ppermute | solution.py:350
  41.7 5.5 %collective-permute-start.9 = (f32[136,128]{1,0:T(8,128)S(1)}, f32[136,128]{1,0:T(8,128)S(1)}, u32[]{:S(2)}, u32[]{:S(2)}) collective-permute-start(f32[136,128]{1,0:T(8,128)S(1)} %multiply_select_fusion.refs_0_), channel_id=1, source_target_pairs={{0,24},{4,28},{8,0},{12,4},{16,8},{20,12},{24,16},{28,20},{1,25},{... | collective-permute-start | bytes 208904 | tf_op jit(solution)/shard_map/ppermute | solution.py:350
  43.9 4.3 %collective-permute-start.10 = (f32[136,128]{1,0:T(8,128)S(1)}, f32[136,128]{1,0:T(8,128)S(1)}, u32[]{:S(2)}, u32[]{:S(2)}) collective-permute-start(f32[136,128]{1,0:T(8,128)S(1)} %multiply_select_fusion.refs_0_), channel_id=1, source_target_pairs={{0,28},{4,0},{8,4},{12,8},{16,12},{20,16},{24,20},{28,24},{1,29},{... | collective-permute-start | bytes 208904 | tf_op jit(solution)/shard_map/ppermute | solution.py:350

commit v4 on v3

--- a/solution.py
+++ b/solution.py
@@ -57,15 +57,15 @@
     )
 
 
-def prep_kernel(
-    C, edges_ref, side_ref, lines_ref, *refs
-):
-    sources, refs = refs[:5], refs[5:]
-    (coarse_ref, fine_ref, worst_ref, keep_ref, send_ref), held, sems = refs[:5], refs[5:10], refs[10]
+def prep_kernel(C, side_ref, *refs):
+    sources, refs = refs[:7], refs[7:]
+    (coarse_ref, fine_ref, worst_ref, keep_ref, send_ref), held, sems = refs[:5], refs[5:12], refs[12]
     copies = [pltpu.make_async_copy(src, dst, sems.at[i]) for i, (src, dst) in enumerate(zip(sources, held))]
     for copy in copies:
         copy.start()
-    ids_ref, a_ref, b_ref, c_ref, d_ref = held
+    edges_ref, lines_ref, ids_ref, a_ref, b_ref, c_ref, d_ref = held
+    copies[0].wait()
+    copies[1].wait()
     bins = edges_ref.shape[0]
     cell = lax.broadcasted_iota(jnp.int32, coarse_ref.shape, 0) * LANES + lax.broadcasted_iota(
         jnp.int32, coarse_ref.shape, 1
@@ -93,7 +93,7 @@
     following = jnp.where(last, below, left)
     fine_ref[...] = q + (following - q) * 65536
 
-    for copy in copies:
+    for copy in copies[2:]:
         copy.wait()
     flag = side_ref[0] == 0
     half = C // 2
@@ -118,10 +118,12 @@
 def run_prep(edges, side, ids, a, b, c, d, C):
     bins = edges.shape[0]
     lines = ids.shape[0]
-    smem = pl.BlockSpec(memory_space=pltpu.SMEM)
+    sources = (edges, edges.reshape(-1, LANES), ids, a, b, c, d)
+    sources = [pltpu.with_memory_space_constraint(x, pltpu.HBM) for x in sources]
+    held = [pltpu.SMEM(edges.shape, edges.dtype)] + [pltpu.VMEM(x.shape, x.dtype) for x in sources[1:]]
     return pl.pallas_call(
         functools.partial(prep_kernel, C),
-        in_specs=[smem, smem, pl.BlockSpec(memory_space=pltpu.VMEM)] + [pl.BlockSpec(memory_space=pltpu.HBM)] * 5,
+        in_specs=[pl.BlockSpec(memory_space=pltpu.SMEM)] + [pl.BlockSpec(memory_space=pltpu.HBM)] * 7,
         out_shape=[
             jax.ShapeDtypeStruct((LEAST // 8 // LANES, LANES), jnp.int32),
             jax.ShapeDtypeStruct((bins // LANES, LANES), jnp.int32),
@@ -129,13 +131,13 @@
             jax.ShapeDtypeStruct((3, lines * C // 2, LANES), jnp.float32),
             jax.ShapeDtypeStruct((3, lines * C // 2, LANES), jnp.float32),
         ],
-        scratch_shapes=[pltpu.VMEM(x.shape, x.dtype) for x in (ids, a, b, c, d)] + [pltpu.SemaphoreType.DMA((5,))],
+        scratch_shapes=held + [pltpu.SemaphoreType.DMA((7,))],
         compiler_params=pltpu.CompilerParams(vmem_limit_bytes=VMEM),
         name="prep",
-    )(edges, side, pltpu.with_memory_space_constraint(edges.reshape(-1, LANES), pltpu.HBM), ids, a, b, c, d)
-
-
-def hist_kernel(C, KT, n, edges_ref, place_ref, coarse_ref, fine_ref, slack_ref, *refs):
+    )(side, *sources)
+
+
+def hist_kernel(C, KT, n, place_ref, coarse_ref, fine_ref, slack_ref, *refs):
     if n:
         prior_ref, prior_low_ref = refs[:2]
         outs, (low_ref, buf0, buf1, all_ref) = refs[2:2 + n], refs[2 + n:]
@@ -145,7 +147,7 @@
     nblk = fine_ref.shape[0]
     lines = KT * C
     chunks = slack_ref.shape[1] // lines
-    x0 = edges_ref[0].astype(jnp.float32) * jnp.float32(STEP)
+    x0 = ((fine_ref[:1, :1] & 0xFFFF) - LEAST).astype(jnp.float32) * jnp.float32(STEP)
 
     def body(*accs):
         for a in accs:
@@ -262,13 +264,13 @@
             at = i * chunk_rows + hist_rows
             all_ref[at:at + EXTRA, :] = tile
         for d in range(n):
-            at = pl.multiple_of(lax.rem(place_ref[0] + d, n) * chunk_rows, 8)
+            at = pl.multiple_of((place_ref[0] ^ d) * chunk_rows, 8)
             outs[d][...] = all_ref[pl.ds(at, chunk_rows), :]
 
     pl.run_scoped(body, *[pltpu.ACC(s % 2)((LANES + 16, 256), jnp.float32) for s in range(series)])
 
 
-def run_hist(edges, place, coarse, fine, slack, C, n=0, prior=(), KT=16):
+def run_hist(place, coarse, fine, slack, C, n=0, prior=(), KT=16):
     nblk = fine.shape[0]
     series = 2 * C
     smem = pl.BlockSpec(memory_space=pltpu.SMEM)
@@ -284,7 +286,7 @@
         outs = [jax.ShapeDtypeStruct((series, LANES + 16, nblk * GROUPS), jnp.float32)]
     return pl.pallas_call(
         functools.partial(hist_kernel, C, KT, n),
-        in_specs=[smem, smem] + [vm] * (3 + len(prior)),
+        in_specs=[smem] + [vm] * (3 + len(prior)),
         out_shape=outs + [low],
         scratch_shapes=scratch,
         cost_estimate=pl.CostEstimate(
@@ -292,7 +294,7 @@
         ),
         compiler_params=pltpu.CompilerParams(vmem_limit_bytes=VMEM),
         name="hist",
-    )(edges, place, coarse, fine, slack, *prior)
+    )(place, coarse, fine, slack, *prior)
 
 
 def final_kernel(C, own, share, scale, me_ref, *refs):
@@ -302,7 +304,7 @@
     half = C // 2
     each = hist_ref.shape[0] // GROUPS // 2
     for d in range(n):
-        source = lax.rem(me_ref[0] - d + n, n)
+        source = me_ref[0] ^ d
         place, side = source >> 1, source & 1
         for p in range(own):
             at = pl.multiple_of((place * own + p) * 2 * each + side * each, 8)
@@ -350,6 +352,20 @@
     return lax.ppermute(value, axis, [(i, (i + distance) % size) for i in range(size)])
 
 
+def turned(index, odd):
+    return jnp.where(odd, (index & ~3) | ((index & 1) << 1) | ((index >> 1) & 1), index)
+
+
+def moved(value, target):
+    n, blocks = lax.axis_size("ep"), lax.axis_size("corner")
+
+    def place(i, k):
+        return (i & ~3 | (i & 1) << 1 | (i >> 1) & 1) if k % 2 else i
+
+    pairs = [(place(i, k) * blocks + k, place(target(i), k) * blocks + k) for i in range(n) for k in range(blocks)]
+    return lax.ppermute(value, ("ep", "corner"), pairs)
+
+
 def tiles(x):
     c, e = x.shape
     return x.reshape(c, e // LANES, LANES).transpose(1, 0, 2).reshape(-1, LANES)
@@ -359,7 +375,7 @@
     C, rows = required.shape
     bins = bin_edges.shape[0]
     n = lax.axis_size("ep")
-    me = lax.axis_index("ep")
+    me = turned(lax.axis_index("ep"), lax.axis_index("corner") % 2 == 1)
     endpoints = rows * n
     density = GROUPS * bins / endpoints
     half = C // 2
@@ -368,15 +384,12 @@
     rest = n // 2
     data = (tiles(required), tiles(arrival), tiles(early_arrival), tiles(hold_required))
     ids = part_ids.reshape(-1, LANES)
-    data = tuple(pltpu.with_memory_space_constraint(x, pltpu.HBM) for x in data)
     lines = ids.shape[0]
-    coarse, fine, near, keep, send = run_prep(bin_edges, side.reshape(1), pltpu.with_memory_space_constraint(ids, pltpu.HBM), *data, C)
-    got = lax.ppermute(send, "ep", [(i, i ^ 1) for i in range(n)])
+    coarse, fine, near, keep, send = run_prep(bin_edges, side.reshape(1), ids, *data, C)
+    got = moved(send, lambda i: i ^ 1)
+    prior = run_hist(place.reshape(1), coarse, fine, keep, half)
+    chunks = run_hist(place.reshape(1), coarse, fine, got, half, rest, prior)
     shares = [rotate(near, "corner", d) for d in range(1, lax.axis_size("corner"))]
-    prior = run_hist(bin_edges, place.reshape(1), coarse, fine, keep, half)
-    chunks = run_hist(bin_edges, place.reshape(1), coarse, fine, got, half, rest, prior)
-    worst = functools.reduce(jnp.minimum, shares, near).reshape(lines, 2, LANES)
-    worst = worst.transpose(1, 0, 2).reshape(2, rows)
 
     own = GROUPS // rest
     nblk = bins // LANES
@@ -386,11 +399,20 @@
     row = lax.broadcasted_iota(jnp.int32, total.shape, 0)
     lane = lax.broadcasted_iota(jnp.int32, total.shape, 1)
     least = (row >= hrows) & (row < hrows + 2 * half) & (lane >= GROUPS)
-    for d in range(1, rest):
-        piece = rotate(chunks[d], "ep", 2 * d)
+    order = sorted(range(1, rest), key=lambda d: (-(d & -2), d))
+    for d in order:
+        piece = moved(chunks[d], lambda i: i ^ 2 * d)
         total = jnp.where(least, jnp.minimum(total, piece), total + piece)
     mine = jnp.where(row < hrows, total * density, total)
-    pieces = [rotate(mine, "ep", d) if d else mine for d in range(n)]
+    pieces = [mine] + [None] * (n - 1)
+    for d in range(1, rest):
+        pieces[2 * d] = moved(mine, lambda i: i ^ 2 * d)
+    pieces[1] = moved(mine, lambda i: i ^ 1)
+    for d in range(1, rest):
+        pieces[2 * d + 1] = moved(pieces[2 * d], lambda i: i ^ 1)
+    worst = functools.reduce(jnp.minimum, shares, near)
+    worst = worst.reshape(lines, 2, LANES)
+    worst = worst.transpose(1, 0, 2).reshape(2, rows)
     full, part_tns, part_share, tns, wns = run_final(me.reshape(1), pieces, C, own, 2 * each, endpoints)
     part_hist = full.reshape(GROUPS, C, nblk, 2, LANES).transpose(0, 1, 3, 2, 4).reshape(GROUPS, C, 2, bins)
     part_tns = part_tns.transpose(2, 0, 1)

time: 49.4 us -> 46 us (0.931)
  starting transfers between devices: 20.8 us -> 17.1 us
  waiting for transfers between devices: 9.83 us -> 12.2 us
  Pallas kernels: 16.2 us -> 14.9 us
  local copies, waits for them, and re-layouts: 0.68 us -> 0 us
    ppermute x13 -> x3, starting transfers between devices: 19.3 us -> 3.13 us  [rotate(): lax.ppermute(value, axis, [(i, (i + distance) % size) for i in range(size)])]
    ppermute x1 -> x11, starting transfers between devices: 1.49 us -> 14 us  [moved(): return lax.ppermute(value, ('ep', 'corner'), pairs)]
    ppermute x1 -> x11, waiting for transfers between devices: 2.52 us -> 12.2 us  [moved(): return lax.ppermute(value, ('ep', 'corner'), pairs)]
    ppermute x13 -> x3, waiting for transfers between devices: 7.31 us -> 0.01 us  [rotate(): lax.ppermute(value, axis, [(i, (i + distance) % size) for i in range(size)])]
    pallas_call x3, Pallas kernels: 15.3 us -> 14.1 us  [the longest x2 12.1 us: run_hist(): pl.pallas_call(functools.partial(hist_kernel, C, KT, n), in_specs=[smem]...]
    unnamed x2 -> x0, local copies, waits for them, and re-layouts: 0.68 us -> none
  transfers between devices with their start and end apart: 14 -> 14, of which waited for: 6 -> 8; matrix products, arithmetic and copies ran while one was open for 2% -> 2% of each run, Pallas kernels for 27% -> 26%
where the time goes in v4:
time: 46 us; the launch traced here: 45.9 us
  starting transfers between devices  17.1 us (37%)
  Pallas kernels  14.9 us (32%)
  waiting for transfers between devices  12.2 us (27%)
  other arithmetic  0.91 us (2%)
  between operations  0.72 us (2%)
    ppermute x11, starting transfers between devices, moved(): return lax.ppermute(value, ('ep', 'corner'), pairs)  14 us
    ppermute x11, waiting for transfers between devices, moved(): return lax.ppermute(value, ('ep', 'corner'), pairs)  12.2 us
    pallas_call x2, Pallas kernels, run_hist(): pl.pallas_call(functools.partial(hist_kernel, C, KT, n), in_specs=[smem]...  12.1 us
    ppermute x3, starting transfers between devices, rotate(): lax.ppermute(value, axis, [(i, (i + distance) % size) for i in range(size)])  3.13 us
    pallas_call x1, Pallas kernels, run_prep(): pl.pallas_call(functools.partial(prep_kernel, C), in_specs=[pl.BlockSpec(...  1.99 us
  transfers between devices with their start and end apart: 14, of which 8 were waited for; matrix products, arithmetic and copies ran while one was open for 2% of the time, Pallas kernels for 26%

profile of v4, /device:TPU:0, one launch (start us, length us, event | category | flops | bytes accessed | tf_op | source)
XLA Modules:
  0.0 45.9 jit_solution(11662849961407633096)
XLA Ops:
  0.7 2.0 %prep.1 = (s32[4,128]{1,0:T(4,128)S(1)}, s32[4,128]{1,0:T(4,128)S(1)}, f32[512,128]{1,0:T(8,128)S(1)}, f32[3,256,128]{2,1,0:T(8,128)S(1)}, f32[3,256,128]{2,1,0:T(8,128)S(1)}) custom-call(s32[1]{0:T(128)} %bitcast.2.side_ref, s32[512]{0:T(512)} %refs_0_.1, s32[4,128]{1,0:T(4,128)} %bitcast.43, s32[256,128]{1,0:T(8,128)} %bitcast.42, f32[512,128]{1,0:T(8,128)} %bitcast.38, ...), custom_call_target="tpu_custom_call" | custom-call | tf_op jit(solution)/shard_map/prep/pallas_call | solution.py:124
  2.7 2.5 %collective-permute-start.13 = (f32[512,128]{1,0:T(8,128)S(1)}, f32[512,128]{1,0:T(8,128)S(1)}, u32[]{:S(2)}, u32[]{:S(2)}) collective-permute-start(f32[512,128]{1,0:T(8,128)S(1)} %get-tuple-element.37), channel_id=1, source_target_pairs={{0,3},{1,0},{2,1},{3,2},{4,7},{5,4},{6,5},{7,6},{8,11},{9,8},{10,9... | collective-permute-start | bytes 786440 | tf_op jit(solution)/shard_map/ppermute | solution.py:352
  5.2 0.6 %collective-permute-start.12 = (f32[512,128]{1,0:T(8,128)S(1)}, f32[512,128]{1,0:T(8,128)S(1)}, u32[]{:S(2)}, u32[]{:S(2)}) collective-permute-start(f32[512,128]{1,0:T(8,128)S(1)} %get-tuple-element.37), channel_id=1, source_target_pairs={{0,2},{1,3},{2,0},{3,1},{4,6},{5,7},{6,4},{7,5},{8,10},{9,11},{10,... | collective-permute-start | bytes 786440 | tf_op jit(solution)/shard_map/ppermute | solution.py:352
  5.8 1.5 %collective-permute-start = (f32[3,256,128]{2,1,0:T(8,128)S(1)}, f32[3,256,128]{2,1,0:T(8,128)S(1)}, u32[]{:S(2)}, u32[]{:S(2)}) collective-permute-start(f32[3,256,128]{2,1,0:T(8,128)S(1)} %get-tuple-element.24), channel_id=1, source_target_pairs={{0,4},{1,9},{2,6},{3,11},{4,0},{9,1},{6,2},{11,3},{8,12},{5,13},{1... | collective-permute-start | bytes 1179656 | tf_op jit(solution)/shard_map/ppermute | solution.py:366
  7.3 5.9 %hist.2 = (f32[2,144,256]{2,1,0:T(8,128)S(1)}, f32[2,8,128]{2,1,0:T(8,128)S(1)}) custom-call(s32[1]{0:T(128)} %bitcast.1.place_ref, s32[4,128]{1,0:T(4,128)S(1)} %get-tuple-element.22.coarse_ref, s32[4,128]{1,0:T(4,128)S(1)} %get-tuple-element.23.fine_ref, f32[3,256,128]{2,1,0:T(8,128)S(1)} %get-tuple-element.25.slack_ref), custom_call_target="tpu_custom_call" | custom-call | flops 4831838208 | bytes 786432 | tf_op jit(solution)/shard_map/hist/pallas_call | solution.py:287
  13.2 0.3 collective-permute-done.slack_ref
  13.6 6.2 %hist.3 = (f32[136,128]{1,0:T(8,128)S(1)}, f32[136,128]{1,0:T(8,128)S(1)}, f32[136,128]{1,0:T(8,128)S(1)}, f32[136,128]{1,0:T(8,128)S(1)}, f32[2,8,128]{2,1,0:T(8,128)}) custom-call(s32[1]{0:T(128)} %bitcast.1.place_ref, s32[4,128]{1,0:T(4,128)S(1)} %get-tuple-element.22.coarse_ref, s32[4,128]{1,0:T(4,128)S(1)} %get-tuple-element.23.fine_ref, ...), custom_call_target="tpu_custom_call" | custom-call | flops 4831838208 | bytes 786432 | tf_op jit(solution)/shard_map/hist/pallas_call | solution.py:287
  19.7 1.6 %collective-permute-start.3 = (f32[136,128]{1,0:T(8,128)S(1)}, f32[136,128]{1,0:T(8,128)S(1)}, u32[]{:S(2)}, u32[]{:S(2)}) collective-permute-start(f32[136,128]{1,0:T(8,128)S(1)} %get-tuple-element.31), channel_id=1, source_target_pairs={{0,8},{1,5},{2,10},{3,7},{4,12},{9,13},{6,14},{11,15},{8,0},{5,1},... | collective-permute-start | bytes 208904 | tf_op jit(solution)/shard_map/ppermute | solution.py:366
  21.4 2.5 %collective-permute-start.2 = (f32[136,128]{1,0:T(8,128)S(1)}, f32[136,128]{1,0:T(8,128)S(1)}, u32[]{:S(2)}, u32[]{:S(2)}) collective-permute-start(f32[136,128]{1,0:T(8,128)S(1)} %get-tuple-element.30), channel_id=1, source_target_pairs={{0,24},{1,21},{2,26},{3,23},{4,28},{9,29},{6,30},{11,31},{8,16},{5... | collective-permute-start | bytes 208904 | tf_op jit(solution)/shard_map/ppermute | solution.py:366
  23.9 0.1 collective-permute-start.1
  24.0 0.1 collective-permute-done.3
  24.1 0.0 collective-permute-start.11
  24.1 3.8 %collective-permute-done.2 = f32[136,128]{1,0:T(8,128)S(1)} collective-permute-done((f32[136,128]{1,0:T(8,128)S(1)}, f32[136,128]{1,0:T(8,128)S(1)}, u32[]{:S(2)}, u32[]{:S(2)}) %collective-permute-start.2) | collective-permute-done | bytes 69664 | tf_op jit(solution)/shard_map/ppermute | solution.py:366
  28.0 2.2 %collective-permute-done.1 = f32[136,128]{1,0:T(8,128)S(1)} collective-permute-done((f32[136,128]{1,0:T(8,128)S(1)}, f32[136,128]{1,0:T(8,128)S(1)}, u32[]{:S(2)}, u32[]{:S(2)}) %collective-permute-start.1) | collective-permute-done | bytes 69664 | tf_op jit(solution)/shard_map/ppermute | solution.py:366
  30.1 0.1 multiply_select_fusion.refs_0_
  30.2 0.5 collective-permute-start.5
  30.7 3.4 %collective-permute-start.7 = (f32[136,128]{1,0:T(8,128)S(1)}, f32[136,128]{1,0:T(8,128)S(1)}, u32[]{:S(2)}, u32[]{:S(2)}) collective-permute-start(f32[136,128]{1,0:T(8,128)S(1)} %multiply_select_fusion.refs_0_), channel_id=1, source_target_pairs={{0,16},{1,17},{2,18},{3,19},{4,20},{9,25},{6,22},{11,27},{8,24},{5... | collective-permute-start | bytes 208904 | tf_op jit(solution)/shard_map/ppermute | solution.py:366
  34.1 0.0 collective-permute-done.13
  34.1 0.6 %collective-permute-start.9 = (f32[136,128]{1,0:T(8,128)S(1)}, f32[136,128]{1,0:T(8,128)S(1)}, u32[]{:S(2)}, u32[]{:S(2)}) collective-permute-start(f32[136,128]{1,0:T(8,128)S(1)} %multiply_select_fusion.refs_0_), channel_id=1, source_target_pairs={{0,24},{1,21},{2,26},{3,23},{4,28},{9,29},{6,30},{11,31},{8,16},{5... | collective-permute-start | bytes 208904 | tf_op jit(solution)/shard_map/ppermute | solution.py:366
  34.7 0.0 collective-permute-done.12
  34.7 1.5 %collective-permute-start.4 = (f32[136,128]{1,0:T(8,128)S(1)}, f32[136,128]{1,0:T(8,128)S(1)}, u32[]{:S(2)}, u32[]{:S(2)}) collective-permute-start(f32[136,128]{1,0:T(8,128)S(1)} %multiply_select_fusion.refs_0_), channel_id=1, source_target_pairs={{0,4},{1,9},{2,6},{3,11},{4,0},{9,1},{6,2},{11,3},{8,12},{5,13},{1... | collective-permute-start | bytes 208904 | tf_op jit(solution)/shard_map/ppermute | solution.py:366
  36.2 0.0 collective-permute-done.5.refs_2_
  36.2 0.6 %collective-permute-start.6 = (f32[136,128]{1,0:T(8,128)S(1)}, f32[136,128]{1,0:T(8,128)S(1)}, u32[]{:S(2)}, u32[]{:S(2)}) collective-permute-start(f32[136,128]{1,0:T(8,128)S(1)} %collective-permute-done.5.refs_2_), channel_id=1, source_target_pairs={{0,4},{1,9},{2,6},{3,11},{4,0},{9,1},{6,2},{11,3},{8,12},{5,13},{1... | collective-permute-start | bytes 208904 | tf_op jit(solution)/shard_map/ppermute | solution.py:366
  36.8 2.5 %collective-permute-done.7.refs_4_ = f32[136,128]{1,0:T(8,128)S(1)} collective-permute-done((f32[136,128]{1,0:T(8,128)S(1)}, f32[136,128]{1,0:T(8,128)S(1)}, u32[]{:S(2)}, u32[]{:S(2)}) %collective-permute-start.7) | collective-permute-done | bytes 69664 | tf_op jit(solution)/shard_map/ppermute | solution.py:366
  39.2 0.0 collective-permute-start.8
  39.2 1.5 %collective-permute-done.9.refs_6_ = f32[136,128]{1,0:T(8,128)S(1)} collective-permute-done((f32[136,128]{1,0:T(8,128)S(1)}, f32[136,128]{1,0:T(8,128)S(1)}, u32[]{:S(2)}, u32[]{:S(2)}) %collective-permute-start.9) | collective-permute-done | bytes 69664 | tf_op jit(solution)/shard_map/ppermute | solution.py:366
  40.7 1.7 %collective-permute-start.10 = (f32[136,128]{1,0:T(8,128)S(1)}, f32[136,128]{1,0:T(8,128)S(1)}, u32[]{:S(2)}, u32[]{:S(2)}) collective-permute-start(f32[136,128]{1,0:T(8,128)S(1)} %collective-permute-done.9.refs_6_), channel_id=1, source_target_pairs={{0,4},{1,9},{2,6},{3,11},{4,0},{9,1},{6,2},{11,3},{8,12},{5,13},{1... | collective-permute-start | bytes 208904 | tf_op jit(solution)/shard_map/ppermute | solution.py:366
  42.4 0.0 collective-permute-done.11
  42.4 0.8 %minimum_minimum_fusion = f32[512,128]{1,0:T(8,128)} fusion(f32[512,128]{1,0:T(8,128)S(1)} %collective-permute-done.13, f32[512,128]{1,0:T(8,128)S(1)} %collective-permute-done.12, f32[512,128]{1,0:T(8,128)S(1)} %get-tuple-element.37, f32[512,128]{1,0:T(8,128)S(1)} %collective-permute-done.11), kind=kLoop, calls=%fused_computation | loop fusion | flops 196608 | bytes 1310720 | tf_op jit(solution)/shard_map/min | solution.py:413
  43.2 0.0 collective-permute-done.4.refs_1_
  43.2 0.0 collective-permute-done.6.refs_3_
  43.2 0.3 collective-permute-done.8.refs_5_
  43.6 1.5 %collective-permute-done.10.refs_7_ = f32[136,128]{1,0:T(8,128)S(1)} collective-permute-done((f32[136,128]{1,0:T(8,128)S(1)}, f32[136,128]{1,0:T(8,128)S(1)}, u32[]{:S(2)}, u32[]{:S(2)}) %collective-permute-start.10) | collective-permute-done | bytes 69664 | tf_op jit(solution)/shard_map/ppermute | solution.py:366
  45.0 0.9 %final.1 = (f32[1024,128]{1,0:T(8,128)}, f32[2,2,64]{2,1,0:T(2,128)}, f32[1,64]{1,0:T(1,128)}, f32[2,2]{1,0:T(2,128)}, f32[2,2]{1,0:T(2,128)}) custom-call(s32[1]{0:T(128)} %bitcast.me_ref, f32[136,128]{1,0:T(8,128)S(1)} %multiply_select_fusion.refs_0_, f32[136,128]{1,0:T(8,128)S(1)} %collective-permute-done.4.refs_1_, ...), custom_call_target="tpu_custom_call" | custom-call | tf_op jit(solution)/shard_map/final/pallas_call | solution.py:335
  (2 shorter events, 0.0 us)
Async XLA Ops:
  2.7 31.4 %collective-permute-start.13 = (f32[512,128]{1,0:T(8,128)S(1)}, f32[512,128]{1,0:T(8,128)S(1)}, u32[]{:S(2)}, u32[]{:S(2)}) collective-permute-start(f32[512,128]{1,0:T(8,128)S(1)} %get-tuple-element.37), channel_id=1, source_target_pairs={{0,3},{1,0},{2,1},{3,2},{4,7},{5,4},{6,5},{7,6},{8,11},{9,8},{10,9... | collective-permute-start | bytes 786440 | tf_op jit(solution)/shard_map/ppermute | solution.py:352
  5.2 29.6 %collective-permute-start.12 = (f32[512,128]{1,0:T(8,128)S(1)}, f32[512,128]{1,0:T(8,128)S(1)}, u32[]{:S(2)}, u32[]{:S(2)}) collective-permute-start(f32[512,128]{1,0:T(8,128)S(1)} %get-tuple-element.37), channel_id=1, source_target_pairs={{0,2},{1,3},{2,0},{3,1},{4,6},{5,7},{6,4},{7,5},{8,10},{9,11},{10,... | collective-permute-start | bytes 786440 | tf_op jit(solution)/shard_map/ppermute | solution.py:352
  5.8 7.8 %collective-permute-start = (f32[3,256,128]{2,1,0:T(8,128)S(1)}, f32[3,256,128]{2,1,0:T(8,128)S(1)}, u32[]{:S(2)}, u32[]{:S(2)}) collective-permute-start(f32[3,256,128]{2,1,0:T(8,128)S(1)} %get-tuple-element.24), channel_id=1, source_target_pairs={{0,4},{1,9},{2,6},{3,11},{4,0},{9,1},{6,2},{11,3},{8,12},{5,13},{1... | collective-permute-start | bytes 1179656 | tf_op jit(solution)/shard_map/ppermute | solution.py:366
  19.7 4.4 %collective-permute-start.3 = (f32[136,128]{1,0:T(8,128)S(1)}, f32[136,128]{1,0:T(8,128)S(1)}, u32[]{:S(2)}, u32[]{:S(2)}) collective-permute-start(f32[136,128]{1,0:T(8,128)S(1)} %get-tuple-element.31), channel_id=1, source_target_pairs={{0,8},{1,5},{2,10},{3,7},{4,12},{9,13},{6,14},{11,15},{8,0},{5,1},... | collective-permute-start | bytes 208904 | tf_op jit(solution)/shard_map/ppermute | solution.py:366
  21.4 6.6 %collective-permute-start.2 = (f32[136,128]{1,0:T(8,128)S(1)}, f32[136,128]{1,0:T(8,128)S(1)}, u32[]{:S(2)}, u32[]{:S(2)}) collective-permute-start(f32[136,128]{1,0:T(8,128)S(1)} %get-tuple-element.30), channel_id=1, source_target_pairs={{0,24},{1,21},{2,26},{3,23},{4,28},{9,29},{6,30},{11,31},{8,16},{5... | collective-permute-start | bytes 208904 | tf_op jit(solution)/shard_map/ppermute | solution.py:366
  23.9 6.3 %collective-permute-start.1 = (f32[136,128]{1,0:T(8,128)S(1)}, f32[136,128]{1,0:T(8,128)S(1)}, u32[]{:S(2)}, u32[]{:S(2)}) collective-permute-start(f32[136,128]{1,0:T(8,128)S(1)} %get-tuple-element.29), channel_id=1, source_target_pairs={{0,16},{1,17},{2,18},{3,19},{4,20},{9,25},{6,22},{11,27},{8,24},{5... | collective-permute-start | bytes 208904 | tf_op jit(solution)/shard_map/ppermute | solution.py:366
  24.1 18.3 %collective-permute-start.11 = (f32[512,128]{1,0:T(8,128)S(1)}, f32[512,128]{1,0:T(8,128)S(1)}, u32[]{:S(2)}, u32[]{:S(2)}) collective-permute-start(f32[512,128]{1,0:T(8,128)S(1)} %get-tuple-element.37), channel_id=1, source_target_pairs={{0,1},{1,2},{2,3},{3,0},{4,5},{5,6},{6,7},{7,4},{8,9},{9,10},{10,1... | collective-permute-start | bytes 786440 | tf_op jit(solution)/shard_map/ppermute | solution.py:352
  30.2 6.0 %collective-permute-start.5 = (f32[136,128]{1,0:T(8,128)S(1)}, f32[136,128]{1,0:T(8,128)S(1)}, u32[]{:S(2)}, u32[]{:S(2)}) collective-permute-start(f32[136,128]{1,0:T(8,128)S(1)} %multiply_select_fusion.refs_0_), channel_id=1, source_target_pairs={{0,8},{1,5},{2,10},{3,7},{4,12},{9,13},{6,14},{11,15},{8,0},{5,1},... | collective-permute-start | bytes 208904 | tf_op jit(solution)/shard_map/ppermute | solution.py:366
  30.7 8.5 %collective-permute-start.7 = (f32[136,128]{1,0:T(8,128)S(1)}, f32[136,128]{1,0:T(8,128)S(1)}, u32[]{:S(2)}, u32[]{:S(2)}) collective-permute-start(f32[136,128]{1,0:T(8,128)S(1)} %multiply_select_fusion.refs_0_), channel_id=1, source_target_pairs={{0,16},{1,17},{2,18},{3,19},{4,20},{9,25},{6,22},{11,27},{8,24},{5... | collective-permute-start | bytes 208904 | tf_op jit(solution)/shard_map/ppermute | solution.py:366
  34.1 6.6 %collective-permute-start.9 = (f32[136,128]{1,0:T(8,128)S(1)}, f32[136,128]{1,0:T(8,128)S(1)}, u32[]{:S(2)}, u32[]{:S(2)}) collective-permute-start(f32[136,128]{1,0:T(8,128)S(1)} %multiply_select_fusion.refs_0_), channel_id=1, source_target_pairs={{0,24},{1,21},{2,26},{3,23},{4,28},{9,29},{6,30},{11,31},{8,16},{5... | collective-permute-start | bytes 208904 | tf_op jit(solution)/shard_map/ppermute | solution.py:366
  34.7 8.5 %collective-permute-start.4 = (f32[136,128]{1,0:T(8,128)S(1)}, f32[136,128]{1,0:T(8,128)S(1)}, u32[]{:S(2)}, u32[]{:S(2)}) collective-permute-start(f32[136,128]{1,0:T(8,128)S(1)} %multiply_select_fusion.refs_0_), channel_id=1, source_target_pairs={{0,4},{1,9},{2,6},{3,11},{4,0},{9,1},{6,2},{11,3},{8,12},{5,13},{1... | collective-permute-start | bytes 208904 | tf_op jit(solution)/shard_map/ppermute | solution.py:366
  36.2 7.0 %collective-permute-start.6 = (f32[136,128]{1,0:T(8,128)S(1)}, f32[136,128]{1,0:T(8,128)S(1)}, u32[]{:S(2)}, u32[]{:S(2)}) collective-permute-start(f32[136,128]{1,0:T(8,128)S(1)} %collective-permute-done.5.refs_2_), channel_id=1, source_target_pairs={{0,4},{1,9},{2,6},{3,11},{4,0},{9,1},{6,2},{11,3},{8,12},{5,13},{1... | collective-permute-start | bytes 208904 | tf_op jit(solution)/shard_map/ppermute | solution.py:366
  39.2 4.3 %collective-permute-start.8 = (f32[136,128]{1,0:T(8,128)S(1)}, f32[136,128]{1,0:T(8,128)S(1)}, u32[]{:S(2)}, u32[]{:S(2)}) collective-permute-start(f32[136,128]{1,0:T(8,128)S(1)} %collective-permute-done.7.refs_4_), channel_id=1, source_target_pairs={{0,4},{1,9},{2,6},{3,11},{4,0},{9,1},{6,2},{11,3},{8,12},{5,13},{1... | collective-permute-start | bytes 208904 | tf_op jit(solution)/shard_map/ppermute | solution.py:366
  40.7 4.3 %collective-permute-start.10 = (f32[136,128]{1,0:T(8,128)S(1)}, f32[136,128]{1,0:T(8,128)S(1)}, u32[]{:S(2)}, u32[]{:S(2)}) collective-permute-start(f32[136,128]{1,0:T(8,128)S(1)} %collective-permute-done.9.refs_6_), channel_id=1, source_target_pairs={{0,4},{1,9},{2,6},{3,11},{4,0},{9,1},{6,2},{11,3},{8,12},{5,13},{1... | collective-permute-start | bytes 208904 | tf_op jit(solution)/shard_map/ppermute | solution.py:366
